TPU v7x, 32 devices: a whole 2x2x4 slice. The times are simulated.
32 devices in a mesh: section: 2 (over core), seq: 4 (over z), head: 4 (over y, x).
Axes of the slice: x: 2, y: 2, z: 4, core: 2. Of those that a mesh axis runs over, the one named last changes fastest.
Arguments:
- inputs: bfloat16 [2, 1024, 1536], P(None, 'seq'), may hold values from -6 to 6
- segments: int32 [2, 1024], P(None, 'seq'), may hold values from 0 to 31, never falling along the last dimension, each value on 1 to 768 neighbouring positions
- norms: float32 [2, 2, 1536], P('section'), may hold values from 0.25 to 1.75
- rec_in: bfloat16 [1536, 2, 2048], P(None, None, 'head'), may hold values from -0.15625 to 0.15625
- rec_gates: bfloat16 [16, 128, 2, 128], P('head'), may hold values from -0.5 to 0.5
- rec_chan: float32 [8, 2048], P(None, 'head'), may hold values from -20 to 4
- rec_out: bfloat16 [2048, 1536], P('head'), may hold values from -0.125 to 0.125
- attn_q: bfloat16 [1536, 1536], P(None, 'head'), may hold values from -0.15625 to 0.15625
- attn_kv: bfloat16 [1536, 256], replicated, may hold values from -0.15625 to 0.15625
- attn_out: bfloat16 [1536, 1536], P('head'), may hold values from -0.4375 to 0.4375
- mlp_in: bfloat16 [2, 1536, 2, 4608], P('section', None, None, 'head'), may hold values from -0.15625 to 0.15625
- mlp_out: bfloat16 [2, 4608, 1536], P('section', 'head'), may hold values from -0.09375 to 0.09375
- cotangent: bfloat16 [2, 1024, 1536], P(None, 'seq'), may hold values from -6 to 6
Outputs:
- final_out: bfloat16 [2, 1024, 1536], P('section', 'seq')
- grad_inputs: float32 [2, 1024, 1536], P('section', 'seq')
- grad_norms: float32 [2, 2, 1536], P('section', None, 'seq')
- grad_rec_in: float32 [1536, 2, 2048], P(('section', 'seq'), None, 'head')
- grad_rec_gates: float32 [16, 128, 2, 128], P('head', ('section', 'seq'))
- grad_rec_chan: float32 [8, 2048], P('section', 'head')
- grad_rec_out: float32 [2048, 1536], P('head', ('section', 'seq'))
- grad_attn_q: float32 [1536, 1536], P(('section', 'seq'), 'head')
- grad_attn_kv: float32 [1536, 256], P(('section', 'seq'))
- grad_attn_out: float32 [1536, 1536], P('head', ('section', 'seq'))
- grad_mlp_in: float32 [2, 1536, 2, 4608], P('section', 'seq', None, 'head')
- grad_mlp_out: float32 [2, 4608, 1536], P('section', 'head', 'seq')
Inputs may be any that keep to these rules, and one draw needn't show every extreme that they name: `segments`: along each stream segment numbers never fall and rise by one at each new document; a document holds 1 to 768 tokens, and one in every stream holds exactly 768.
All inputs are finite; a program needn't handle non-finite values.
Results may differ from a plain program's by a relative error of at most 0.03.
Values may be sent and summed in bfloat16 or wider, within the bound.
A program may use at most 320 MiB of HBM per device.

v0:
```python
import jax
import jax.numpy as jnp
from jax import lax
from jax.sharding import PartitionSpec as P

WINDOW = 1024


epsilon = 1e-06


def from_behind(array, axis, by):
    devices = lax.axis_size(axis)
    pairs = [(i, i + by) for i in range(devices) if 0 <= i + by < devices]
    return lax.ppermute(array, axis, pairs)


def entering_2(array, axis, combine, identity, reverse):
    devices, position = (lax.axis_size(axis), lax.axis_index(axis))
    everything = jax.tree.map(lambda part: lax.all_gather(part, axis), array)
    start = jax.tree.map(
        lambda part, zero: jnp.broadcast_to(jnp.asarray(zero, part.dtype), part.shape),
        array,
        identity,
    )

    def lap(k, before):
        at = devices - 1 - k if reverse else k
        reached = at > position if reverse else at < position
        new = combine(before, jax.tree.map(lambda part: part[at], everything))
        return jax.tree.map(lambda a, b: jnp.where(reached, a, b), new, before)

    return lax.fori_loop(0, devices, lap, start)


def root_norm(tensor, scale_gain):
    return (
        tensor * lax.rsqrt(jnp.mean(tensor * tensor, axis=-1, keepdims=True) + epsilon) * scale_gain
    )


def norm_back(tensor, scale_gain, upstream):
    gain_rows = jnp.broadcast_to(scale_gain, (tensor.shape[0], scale_gain.shape[0]))
    _, pull_back = jax.vjp(
        lambda tensor_in, gains_in: root_norm(tensor_in, gains_in[:, None, :]), tensor, gain_rows
    )
    return pull_back(upstream)


def gate_math(pre_rate, pre_input, conv_in, lam_param):
    log_decay = -8.0 * jax.nn.sigmoid(pre_rate) * jax.nn.softplus(lam_param)
    decays = jnp.exp(log_decay)
    drive = jnp.sqrt(-jnp.expm1(2.0 * log_decay)) * jax.nn.sigmoid(pre_input) * conv_in
    return (decays, drive)


def affine(earlier, later):
    return (earlier[0] * later[0], later[0] * earlier[1] + later[1])


def head_total(partial_value):
    return lax.psum(partial_value, "head")


def conv_apply(extended, ext_ids, chan_params):
    count = extended.shape[1] - 3
    own_ids = ext_ids[:, 3:]
    total = chan_params[4] + chan_params[0] * extended[:, 3:]
    for offset in range(1, 4):
        same = (ext_ids[:, 3 - offset : 3 - offset + count] == own_ids).astype(jnp.float32)[
            :, :, None
        ]
        total = total + chan_params[offset] * extended[:, 3 - offset : 3 - offset + count] * same
    return total


def feed_forward(residual, scale_gain, w_in, w_out):
    normed = root_norm(residual, scale_gain).astype(jnp.bfloat16)
    gate_up = jnp.einsum("mtd,dkf->mtkf", normed, w_in, preferred_element_type=jnp.float32)
    hidden = (jax.nn.gelu(gate_up[:, :, 0]) * gate_up[:, :, 1]).astype(jnp.bfloat16)
    branch = head_total(
        jnp.einsum("mtf,fd->mtd", hidden, w_out, preferred_element_type=jnp.float32)
    )
    return (residual + branch, (residual, normed, gate_up, hidden))


def feed_back(saved, scale_gain, w_in, w_out, upstream):
    residual, normed, gate_up, hidden = saved
    out_low = upstream.astype(jnp.bfloat16)
    grad_hidden = jnp.einsum("mtd,fd->mtf", out_low, w_out, preferred_element_type=jnp.float32)
    _, pull_back = jax.vjp(
        lambda pair_in: jax.nn.gelu(pair_in[:, :, 0]) * pair_in[:, :, 1], gate_up
    )
    gate_low = pull_back(grad_hidden)[0].astype(jnp.bfloat16)
    grad_normed = head_total(
        jnp.einsum("mtkf,dkf->mtd", gate_low, w_in, preferred_element_type=jnp.float32)
    )
    grad_residual, grad_gain = norm_back(residual, scale_gain, grad_normed)
    return (upstream + grad_residual, grad_gain, ((normed, gate_low), (hidden, out_low)))


def ffn_terms(ffn_pairs, chosen):
    (ffn_normed, gate_low), (hidden, out_low) = ffn_pairs
    grad_in = jnp.einsum(
        "mtd,mtkf->dkf", ffn_normed[chosen], gate_low[chosen], preferred_element_type=jnp.float32
    )
    grad_out = jnp.einsum(
        "mtf,mtd->fd", hidden[chosen], out_low[chosen], preferred_element_type=jnp.float32
    )
    return (grad_in, grad_out)


def section_view(gradient, axis_pos):
    dims_in = gradient.shape
    return gradient.reshape(
        dims_in[:axis_pos] + (2, dims_in[axis_pos] // 2) + dims_in[axis_pos + 1 :]
    )


def seq_sum(parts):
    return (
        lax.psum_scatter(
            parts[0].astype(jnp.bfloat16), "seq", scatter_dimension=1, tiled=True
        ).astype(jnp.float32),
        lax.psum_scatter(
            parts[1].astype(jnp.bfloat16), "seq", scatter_dimension=1, tiled=True
        ).astype(jnp.float32),
        lax.psum_scatter(
            parts[2].astype(jnp.bfloat16), "seq", scatter_dimension=2, tiled=True
        ).astype(jnp.float32),
        lax.psum_scatter(
            parts[3].astype(jnp.bfloat16), "seq", scatter_dimension=0, tiled=True
        ).astype(jnp.float32),
        lax.psum_scatter(
            parts[4].astype(jnp.bfloat16), "seq", scatter_dimension=1, tiled=True
        ).astype(jnp.float32),
        lax.psum_scatter(
            parts[5].astype(jnp.bfloat16), "seq", scatter_dimension=1, tiled=True
        ).astype(jnp.float32),
    )


def reduce_terms(term_fn, pairs, gain_grads, micro_count):
    totals = None
    for micro_index in range(micro_count):
        reduced = seq_sum(term_fn(pairs, gain_grads, slice(micro_index, micro_index + 1)))
        if totals is None:
            totals = reduced
        else:
            totals = tuple(
                (first_sum + second_sum for first_sum, second_sum in zip(totals, reduced))
            )
    return totals


def rec_terms(pairs, gain_grads, chosen):
    (normed, branch_low), (mixed_out, mix_low), (conv_blocks, gate_blocks), ffn_pairs = pairs
    grad_in = jnp.einsum(
        "mtd,mtkr->dkr", normed[chosen], branch_low[chosen], preferred_element_type=jnp.float32
    )
    grad_gates = jnp.einsum(
        "mtnb,mtknc->bnkc",
        conv_blocks[chosen],
        gate_blocks[chosen],
        preferred_element_type=jnp.float32,
    )
    grad_out = jnp.einsum(
        "mtr,mtd->rd", mixed_out[chosen], mix_low[chosen], preferred_element_type=jnp.float32
    )
    ffn_in, ffn_out = ffn_terms(ffn_pairs, chosen)
    return (
        section_view(grad_in, 0),
        section_view(grad_gates, 0),
        section_view(grad_out, 1),
        ffn_in,
        ffn_out,
        jnp.sum(gain_grads[chosen], axis=0),
    )


def attn_terms(pairs, gain_grads, chosen):
    (normed, query_low), (kv_low, attended, out_low), ffn_pairs = pairs
    grad_query = jnp.einsum(
        "mtd,mtq->dq", normed[chosen], query_low[chosen], preferred_element_type=jnp.float32
    )
    grad_kv = jnp.einsum(
        "mtd,mtk->dk", normed[chosen], kv_low[chosen], preferred_element_type=jnp.float32
    )
    grad_out = jnp.einsum(
        "mtq,mtd->qd", attended[chosen], out_low[chosen], preferred_element_type=jnp.float32
    )
    ffn_in, ffn_out = ffn_terms(ffn_pairs, chosen)
    return (
        section_view(grad_query, 0),
        section_view(grad_kv, 0),
        section_view(grad_out, 1),
        ffn_in,
        ffn_out,
        jnp.sum(gain_grads[chosen], axis=0),
    )


def rec_forward(inputs, segments, norms, rec_in, rec_gates, rec_chan, rec_out, mlp_in, mlp_out):
    micro_count, count, width = inputs.shape
    chans = rec_in.shape[2]
    blocks_here, block_size = (rec_gates.shape[0], rec_gates.shape[1])
    stream = inputs.astype(jnp.float32)
    normed = root_norm(stream, norms[0, 0]).astype(jnp.bfloat16)
    branches = jnp.einsum("mtd,dkr->mtkr", normed, rec_in, preferred_element_type=jnp.float32)
    values = branches[:, :, 0].astype(jnp.bfloat16)
    gate_pre = branches[:, :, 1]
    edge_vals, edge_ids = from_behind(
        (values[:, -3:], segments[:, -3:].astype(jnp.bfloat16)), "seq", 1
    )
    extended = jnp.concatenate([edge_vals, values], axis=1).astype(jnp.float32)
    ext_ids = jnp.concatenate([edge_ids.astype(jnp.int32), segments], axis=1)
    conv_low = conv_apply(extended, ext_ids, rec_chan).astype(jnp.bfloat16)
    conv_blocks = conv_low.reshape(micro_count, count, blocks_here, block_size)
    pre_gates = jnp.einsum(
        "mtnb,nbkc->mtknc", conv_blocks, rec_gates, preferred_element_type=jnp.float32
    ).reshape(micro_count, count, 2, chans)
    keep_mask = (ext_ids[:, 2 : 2 + count] == segments).astype(jnp.float32)[:, :, None]
    decays, drive = gate_math(
        pre_gates[:, :, 0] + rec_chan[5],
        pre_gates[:, :, 1] + rec_chan[6],
        conv_low.astype(jnp.float32),
        rec_chan[7],
    )
    decays = decays * keep_mask
    through, local_state = lax.associative_scan(affine, (decays, drive), axis=1)
    unit = jnp.ones((micro_count, chans), jnp.float32)
    _, entering = entering_2(
        (through[:, -1], local_state[:, -1]), "seq", affine, (unit, jnp.zeros_like(unit)), False
    )
    hidden = local_state + through * entering[:, None]
    mixed_out = (hidden * jax.nn.gelu(gate_pre)).astype(jnp.bfloat16)
    residual = stream + head_total(
        jnp.einsum("mtr,rd->mtd", mixed_out, rec_out, preferred_element_type=jnp.float32)
    )
    final, ffn_saved = feed_forward(residual, norms[0, 1], mlp_in[0], mlp_out[0])
    saved = (
        stream,
        normed,
        gate_pre,
        extended,
        ext_ids,
        conv_blocks,
        pre_gates,
        keep_mask,
        decays,
        entering,
        hidden,
        mixed_out,
        ffn_saved,
    )
    return (final.astype(jnp.bfloat16), saved)


def rec_backward(saved, grad_passed, norms, rec_in, rec_gates, rec_chan, rec_out, mlp_in, mlp_out):
    (
        stream,
        normed,
        gate_pre,
        extended,
        ext_ids,
        conv_blocks,
        pre_gates,
        keep_mask,
        decays,
        entering,
        hidden,
        mixed_out,
        ffn_saved,
    ) = saved
    micro_count, count, chans = hidden.shape
    blocks_here, block_size = (rec_gates.shape[0], rec_gates.shape[1])
    grad_res, gain_two, ffn_pairs = feed_back(
        ffn_saved, norms[0, 1], mlp_in[0], mlp_out[0], grad_passed.astype(jnp.float32)
    )
    mix_low = grad_res.astype(jnp.bfloat16)
    grad_mixed = jnp.einsum("mtd,rd->mtr", mix_low, rec_out, preferred_element_type=jnp.float32)
    gate_act, pull_gate = jax.vjp(jax.nn.gelu, gate_pre)
    grad_hidden = grad_mixed * gate_act
    grad_gate = pull_gate(grad_mixed * hidden)[0]
    following = jnp.concatenate([decays[:, 1:], jnp.ones_like(decays[:, :1])], axis=1)
    beyond, local_grad = lax.associative_scan(
        affine, (following, grad_hidden), reverse=True, axis=1
    )
    unit = jnp.ones((micro_count, chans), jnp.float32)
    _, arriving = entering_2(
        (decays[:, 0] * beyond[:, 0], decays[:, 0] * local_grad[:, 0]),
        "seq",
        affine,
        (unit, jnp.zeros_like(unit)),
        True,
    )
    grad_state = local_grad + beyond * arriving[:, None]
    earlier_state = jnp.concatenate([entering[:, None], hidden[:, :-1]], axis=1)
    conv_wide = conv_blocks.reshape(micro_count, count, chans).astype(jnp.float32)
    _, pull_rates = jax.vjp(
        gate_math,
        pre_gates[:, :, 0] + rec_chan[5],
        pre_gates[:, :, 1] + rec_chan[6],
        conv_wide,
        rec_chan[7],
    )
    grad_rate, grad_input, grad_conv, grad_lambda = pull_rates(
        (grad_state * earlier_state * keep_mask, grad_state)
    )
    gate_blocks = (
        jnp.stack([grad_rate, grad_input], axis=2)
        .astype(jnp.bfloat16)
        .reshape(micro_count, count, 2, blocks_here, block_size)
    )
    grad_conv = grad_conv + jnp.einsum(
        "mtknc,nbkc->mtnb", gate_blocks, rec_gates, preferred_element_type=jnp.float32
    ).reshape(micro_count, count, chans)
    _, pull_conv = jax.vjp(
        lambda wide_in, chan_in: conv_apply(wide_in, ext_ids, chan_in), extended, rec_chan
    )
    grad_ext, grad_chan = pull_conv(grad_conv)
    from_next = from_behind(grad_ext[:, :3], "seq", -1)
    grad_values = grad_ext[:, 3:] + jnp.pad(from_next, ((0, 0), (count - 3, 0), (0, 0)))
    branch_low = jnp.stack([grad_values, grad_gate], axis=2).astype(jnp.bfloat16)
    grad_normed = head_total(
        jnp.einsum("mtkr,dkr->mtd", branch_low, rec_in, preferred_element_type=jnp.float32)
    )
    grad_stream, gain_one = norm_back(stream, norms[0, 0], grad_normed)
    bias_rows = jnp.stack(
        [jnp.sum(grad_rate, axis=(0, 1)), jnp.sum(grad_input, axis=(0, 1)), grad_lambda]
    )
    chan_grad = grad_chan + jnp.concatenate([jnp.zeros((5, chans), jnp.float32), bias_rows], axis=0)
    pairs = ((normed, branch_low), (mixed_out, mix_low), (conv_blocks, gate_blocks), ffn_pairs)
    return (grad_res + grad_stream, jnp.stack([gain_one, gain_two], axis=1), chan_grad, pairs)


def rec_finish(saved, grad_passed, norms, rec_in, rec_gates, rec_chan, rec_out, mlp_in, mlp_out):
    grad_inputs, gain_grads, chan_grad, pairs = rec_backward(
        saved, grad_passed, norms, rec_in, rec_gates, rec_chan, rec_out, mlp_in, mlp_out
    )
    chan_total = lax.psum(chan_grad, "seq")
    reduced = reduce_terms(rec_terms, pairs, gain_grads, grad_inputs.shape[0])
    stay_half = (reduced[0][0], jnp.swapaxes(reduced[1][0], 0, 1), reduced[2][:, 0], chan_total[:4])
    send_half = (reduced[0][1], jnp.swapaxes(reduced[1][1], 0, 1), reduced[2][:, 1], chan_total[4:])
    return (grad_inputs, stay_half, send_half, (reduced[3], reduced[4], reduced[5]))


def attend(packed):
    query_rows, key_rows, allowed = packed
    head_dim = query_rows.shape[2]
    scores = jnp.einsum(
        "qhd,kd->hqk", query_rows, key_rows[:, :head_dim], preferred_element_type=jnp.float32
    ) * head_dim ** (-0.5)
    masked = jnp.where(allowed[None], scores, -1e30)
    row_max = jnp.max(masked, axis=-1, keepdims=True)
    lifted = jnp.exp(masked - row_max)
    row_total = jnp.sum(lifted, axis=-1, keepdims=True)
    weights = (lifted / row_total).astype(jnp.bfloat16)
    attended = jnp.einsum(
        "hqk,kd->qhd", weights, key_rows[:, head_dim:], preferred_element_type=jnp.float32
    ).astype(jnp.bfloat16)
    return (attended, row_max[:, :, 0] + jnp.log(row_total[:, :, 0]))


def attend_back(packed):
    query_rows, key_rows, allowed, log_total, grad_rows = packed
    head_dim = query_rows.shape[2]
    factor = head_dim ** (-0.5)
    scores = (
        jnp.einsum(
            "qhd,kd->hqk", query_rows, key_rows[:, :head_dim], preferred_element_type=jnp.float32
        )
        * factor
    )
    probs = jnp.exp(jnp.where(allowed[None], scores, -1e30) - log_total[:, :, None])
    weights = probs.astype(jnp.bfloat16)
    grad_probs = jnp.einsum(
        "qhd,kd->hqk", grad_rows, key_rows[:, head_dim:], preferred_element_type=jnp.float32
    )
    grad_values = jnp.einsum("hqk,qhd->kd", weights, grad_rows, preferred_element_type=jnp.float32)
    grad_scores = (
        probs * (grad_probs - jnp.sum(grad_probs * probs, axis=-1, keepdims=True))
    ).astype(jnp.bfloat16)
    grad_query = (
        jnp.einsum(
            "hqk,kd->qhd", grad_scores, key_rows[:, :head_dim], preferred_element_type=jnp.float32
        )
        * factor
    )
    grad_keys = (
        jnp.einsum("hqk,qhd->kd", grad_scores, query_rows, preferred_element_type=jnp.float32)
        * factor
    )
    return (grad_query, jnp.concatenate([grad_keys, grad_values], axis=-1))


def attn_forward(passed, segments, norms, attn_q, attn_kv, attn_out, mlp_in, mlp_out):
    micro_count, count, width = passed.shape
    head_dim = attn_kv.shape[1] // 2
    heads_here = attn_q.shape[1] // head_dim
    stream = passed.astype(jnp.float32)
    normed = root_norm(stream, norms[0, 0]).astype(jnp.bfloat16)
    queries = jnp.einsum("mtd,dq->mtq", normed, attn_q, preferred_element_type=jnp.float32).astype(
        jnp.bfloat16
    )
    keyval = jnp.einsum("mtd,dk->mtk", normed, attn_kv, preferred_element_type=jnp.float32).astype(
        jnp.bfloat16
    )
    reach = max(1, WINDOW // count)
    wire_ids = segments.astype(jnp.bfloat16)
    window_kv, window_ids = ([], [])
    for distance in range(reach, 0, -1):
        got_kv, got_ids = from_behind((keyval, wire_ids), "seq", distance)
        window_kv.append(got_kv)
        window_ids.append(got_ids.astype(jnp.int32))
    all_keys = jnp.concatenate(window_kv + [keyval], axis=1)
    key_ids = jnp.concatenate(window_ids + [segments], axis=1)
    anchor = lax.axis_index("seq") * count
    key_spots = anchor - reach * count + jnp.arange((reach + 1) * count, dtype=jnp.int32)
    query_spots = anchor + jnp.arange(count, dtype=jnp.int32)
    distance_q = query_spots[:, None] - key_spots[None, :]
    inside = (distance_q >= 0) & (distance_q < WINDOW) & (key_spots >= 0)[None, :]
    allowed = inside[None] & (segments[:, :, None] == key_ids[:, None, :])
    query_heads = queries.reshape(micro_count, count, heads_here, head_dim)
    attended, log_totals = lax.map(attend, (query_heads, all_keys, allowed))
    attended = attended.reshape(micro_count, count, heads_here * head_dim)
    residual = stream + head_total(
        jnp.einsum("mtq,qd->mtd", attended, attn_out, preferred_element_type=jnp.float32)
    )
    final, ffn_saved = feed_forward(residual, norms[0, 1], mlp_in[0], mlp_out[0])
    return (
        final,
        (stream, normed, query_heads, all_keys, allowed, attended, log_totals, ffn_saved),
    )


def attn_backward(saved, cotangent, norms, attn_q, attn_kv, attn_out, mlp_in, mlp_out):
    stream, normed, query_heads, all_keys, allowed, attended, log_totals, ffn_saved = saved
    micro_count, count, heads_here, head_dim = query_heads.shape
    width = stream.shape[2]
    grad_res, gain_two, ffn_pairs = feed_back(
        ffn_saved, norms[0, 1], mlp_in[0], mlp_out[0], cotangent.astype(jnp.float32)
    )
    out_low = grad_res.astype(jnp.bfloat16)
    grad_att = jnp.einsum(
        "mtd,qd->mtq", out_low, attn_out, preferred_element_type=jnp.float32
    ).astype(jnp.bfloat16)
    grad_query, grad_kv = lax.map(
        attend_back,
        (
            query_heads,
            all_keys,
            allowed,
            log_totals,
            grad_att.reshape(micro_count, count, heads_here, head_dim),
        ),
    )
    reach = all_keys.shape[1] // count - 1
    own_kv = grad_kv[:, reach * count :]
    for distance in range(1, reach + 1):
        start_row = (reach - distance) * count
        own_kv = own_kv + from_behind(
            grad_kv[:, start_row : start_row + count].astype(jnp.bfloat16), "seq", -distance
        ).astype(jnp.float32)
    query_low = grad_query.reshape(micro_count, count, heads_here * head_dim).astype(jnp.bfloat16)
    joined = head_total(
        jnp.concatenate(
            [
                jnp.einsum("mtq,dq->mtd", query_low, attn_q, preferred_element_type=jnp.float32),
                own_kv,
            ],
            axis=-1,
        )
    )
    kv_low = joined[:, :, width:].astype(jnp.bfloat16)
    grad_normed = joined[:, :, :width] + jnp.einsum(
        "mtk,dk->mtd", kv_low, attn_kv, preferred_element_type=jnp.float32
    )
    grad_stream, gain_one = norm_back(stream, norms[0, 0], grad_normed)
    pairs = ((normed, query_low), (kv_low, attended, out_low), ffn_pairs)
    return (grad_res + grad_stream, jnp.stack([gain_one, gain_two], axis=1), pairs)


def attn_section(arrived, segments, cotangent, norms, attn_q, attn_kv, attn_out, mlp_in, mlp_out):
    final, saved = attn_forward(
        arrived, segments, norms, attn_q, attn_kv, attn_out, mlp_in, mlp_out
    )
    grad_passed, gain_grads, pairs = attn_backward(
        saved, cotangent, norms, attn_q, attn_kv, attn_out, mlp_in, mlp_out
    )
    reduced = reduce_terms(attn_terms, pairs, gain_grads, arrived.shape[0])
    stay_half = (reduced[0][1], reduced[1][1], reduced[2][:, 1])
    send_half = (reduced[0][0], reduced[1][0], reduced[2][:, 0])
    return (
        final.astype(jnp.bfloat16),
        grad_passed.astype(jnp.bfloat16),
        stay_half,
        send_half,
        (reduced[3], reduced[4], reduced[5]),
    )


def only_when(predicate, task_fn):
    result = task_fn()
    return jax.tree.map(lambda value: jnp.where(predicate, value, jnp.zeros_like(value)), result)


def on_device(
    inputs,
    segments,
    norms,
    rec_in,
    rec_gates,
    rec_chan,
    rec_out,
    attn_q,
    attn_kv,
    attn_out,
    mlp_in,
    mlp_out,
    cotangent,
):
    is_first = lax.axis_index("section") == 0
    rec_args = (norms, rec_in, rec_gates, rec_chan, rec_out, mlp_in, mlp_out)
    attn_args = (norms, attn_q, attn_kv, attn_out, mlp_in, mlp_out)
    passed = only_when(is_first, lambda: rec_forward(inputs, segments, *rec_args)[0])
    arrived = from_behind(passed, "section", 1)
    final_all, grad_low, attn_stay, attn_send, attn_ffn = only_when(
        jnp.logical_not(is_first), lambda: attn_section(arrived, segments, cotangent, *attn_args)
    )
    grad_back, final_early = from_behind((grad_low, final_all[0]), "section", -1)
    attn_got = (
        from_behind(attn_send[0].astype(jnp.bfloat16), "section", -1).astype(jnp.float32),
        from_behind(attn_send[1].astype(jnp.bfloat16), "section", -1).astype(jnp.float32),
        from_behind(attn_send[2].astype(jnp.bfloat16), "section", -1).astype(jnp.float32),
    )

    def rec_late():
        rec_saved = rec_forward(inputs, segments, *rec_args)[1]
        return rec_finish(rec_saved, grad_back, *rec_args)

    grad_inputs, rec_stay, rec_send, rec_ffn = only_when(is_first, rec_late)
    rec_got = (
        from_behind(rec_send[0].astype(jnp.bfloat16), "section", 1).astype(jnp.float32),
        from_behind(rec_send[1].astype(jnp.bfloat16), "section", 1).astype(jnp.float32),
        from_behind(rec_send[2].astype(jnp.bfloat16), "section", 1).astype(jnp.float32),
        from_behind(rec_send[3].astype(jnp.bfloat16), "section", 1).astype(jnp.float32),
        from_behind(grad_inputs[1].astype(jnp.bfloat16), "section", 1).astype(jnp.float32),
    )
    output_half = jnp.where(is_first, final_early, final_all[1])[None]
    grad_half = jnp.where(is_first, grad_inputs[0], rec_got[4])[None]
    return (
        output_half,
        grad_half,
        jnp.where(is_first, rec_ffn[2], attn_ffn[2])[None],
        jnp.where(is_first, rec_stay[0], rec_got[0]),
        jnp.where(is_first, rec_stay[1], rec_got[1]),
        jnp.where(is_first, rec_stay[3], rec_got[3]),
        jnp.where(is_first, rec_stay[2], rec_got[2]),
        jnp.where(is_first, attn_got[0], attn_stay[0]),
        jnp.where(is_first, attn_got[1], attn_stay[1]),
        jnp.where(is_first, attn_got[2], attn_stay[2]),
        jnp.where(is_first, rec_ffn[0], attn_ffn[0])[None],
        jnp.where(is_first, rec_ffn[1], attn_ffn[1])[None],
    )


def solution(mesh):
    in_specs = (
        P(None, "seq", None),
        P(None, "seq"),
        P("section", None, None),
        P(None, None, "head"),
        P("head", None, None, None),
        P(None, "head"),
        P("head", None),
        P(None, "head"),
        P(),
        P("head", None),
        P("section", None, None, "head"),
        P("section", "head", None),
        P(None, "seq", None),
    )
    out_specs = (
        P("section", "seq", None),
        P("section", "seq", None),
        P("section", None, "seq"),
        P(("section", "seq"), None, "head"),
        P("head", ("section", "seq"), None, None),
        P("section", "head"),
        P("head", ("section", "seq")),
        P(("section", "seq"), "head"),
        P(("section", "seq"), None),
        P("head", ("section", "seq")),
        P("section", "seq", None, "head"),
        P("section", "head", "seq"),
    )
    return jax.shard_map(
        on_device, mesh=mesh, in_specs=in_specs, out_specs=out_specs, check_vma=False
    )
```

profile of v0, /device:TPU:0, one launch (start us, length us, event | category | flops | bytes accessed | tf_op | source)
XLA Modules:
  0.0 2823.2 jit_solution(1671339069499818410)
XLA Ops:
  259.9 13.7 all-gather
  284.9 14.0 all-gather.1
  314.4 86.3 %all-reduce.93.cloned.1.call-done = f32[2,256,1536]{2,1,0:T(8,128)} async-done(((f32[2,256,1536]{2,1,0:T(8,128)}), f32[2,256,1536]{2,1,0:T(8,128)}) %all-reduce.93.cloned.1.call-update) | async-done | bytes 3145744 | tf_op jit(solution)/shard_map/psum | solution.py:62
  405.4 7.2 fusion.32
  432.2 74.0 %all-reduce.95.cloned.1.call-done = f32[2,256,1536]{2,1,0:T(8,128)} async-done(((f32[2,256,1536]{2,1,0:T(8,128)}), f32[2,256,1536]{2,1,0:T(8,128)}) %all-reduce.95.cloned.1.call-update) | async-done | bytes 3145744 | tf_op jit(solution)/shard_map/psum | solution.py:62
  551.8 13.3 while.59
  569.2 92.7 %all-reduce.97.cloned.1.call-done = f32[2,256,1536]{2,1,0:T(8,128)} async-done(((f32[2,256,1536]{2,1,0:T(8,128)}), f32[2,256,1536]{2,1,0:T(8,128)}) %all-reduce.97.cloned.1.call-update) | async-done | bytes 3145744 | tf_op jit(solution)/shard_map/psum | solution.py:62
  667.6 6.8 fusion.39
  686.5 86.8 %all-reduce.99.cloned.1.call-done = f32[2,256,1536]{2,1,0:T(8,128)} async-done(((f32[2,256,1536]{2,1,0:T(8,128)}), f32[2,256,1536]{2,1,0:T(8,128)}) %all-reduce.99.cloned.1.call-update) | async-done | bytes 3145744 | tf_op jit(solution)/shard_map/psum | solution.py:62
  785.3 28.8 %while.60 = (s32[]{:T(128)}, bf16[2,256,3,128]{1,3,2,0:T(8,128)(2,1)}, f32[2,1280,256]{2,1,0:T(8,128)}, bf16[2,1280,256]{2,1,0:T(8,128)(2,1)}, pred[2,256,1280]{...) while((s32[]{:T(128)}, ...), condition=%wide.region_18.19_spmd, body=%wide.region_16.18_spmd.sunk | while | flops 1267727616 | bytes 52076848 | solution.py:448
  821.8 8.0 collective-permute-done.14
  829.8 9.9 collective-permute-done.13
  843.1 98.6 %all-reduce.101.cloned.1.call-done = f32[2,256,1792]{2,1,0:T(8,128)} async-done(((f32[2,256,1792]{2,1,0:T(8,128)}), f32[2,256,1792]{2,1,0:T(8,128)}) %all-reduce.101.cloned.1.call-update) | async-done | bytes 3670032 | tf_op jit(solution)/shard_map/psum | solution.py:62
  1000.5 7.0 fusion.49
  1007.5 49.6 %all-reduce.103.cloned.1.call-done = f32[2,256,1536]{2,1,0:T(8,128)} async-done(((f32[2,256,1536]{2,1,0:T(8,128)}), f32[2,256,1536]{2,1,0:T(8,128)}) %all-reduce.103.cloned.1.call-update) | async-done | bytes 3145744 | tf_op jit(solution)/shard_map/psum | solution.py:62
  1291.9 8.9 rev.8
  1300.8 8.9 rev.9
  1309.7 14.7 all-gather.2
  1327.1 14.2 all-gather.3
  1349.2 7.0 fusion.271
  1360.1 6.9 fusion.220
  1523.7 7.3 all-reduce.105.cloned.1.call-done
  1539.1 6.5 convolution_convert_fusion
  1552.1 6.4 convolution_convert_fusion.2
  1558.7 6.6 convolution_convert_fusion.3
  1567.7 25.3 reduce-scatter.47.cloned.1.call-done
  1596.9 26.2 reduce-scatter.57.cloned.1.call-done
  1623.1 30.3 %reduce-scatter.55.cloned.1.call-done = bf16[384,2,192]{0,2,1:T(8,128)(2,1)} async-done(((bf16[384,2,768]{0,2,1:T(8,128)(2,1)}), bf16[384,2,192]{0,2,1:T(8,128)(2,1)}) %reduce-scatter.55.cloned.1.call-update) | async-done | bytes 294928 | tf_op jit(solution)/shard_map/reduce_scatter | solution.py:128
  1658.5 62.2 %reduce-scatter.81.cloned.1.call-done = bf16[384,1152]{1,0:T(8,128)(2,1)} async-done(((bf16[1536,1152]{1,0:T(8,128)(2,1)}), bf16[384,1152]{1,0:T(8,128)(2,1)}) %reduce-scatter.81.cloned.1.call-update) | async-done | bytes 884752
  1722.9 66.8 %reduce-scatter.79.cloned.1.call-done = bf16[384,1152]{1,0:T(8,128)(2,1)} async-done(((bf16[1536,1152]{1,0:T(8,128)(2,1)}), bf16[384,1152]{1,0:T(8,128)(2,1)}) %reduce-scatter.79.cloned.1.call-update) | async-done | bytes 884752
  1791.9 21.5 reduce-scatter.73.cloned.1.call-done
  1815.0 19.6 reduce-scatter.71.cloned.1.call-done
  1836.2 22.0 reduce-scatter.53.cloned.1.call-done
  1858.1 24.9 reduce-scatter.51.cloned.1.call-done
  1888.9 18.6 psum.74
  1912.5 11.1 all-reduce.107.cloned.1.call-done
  1927.7 33.5 %reduce-scatter.45.cloned.1.call-done = bf16[512,2,192]{0,2,1:T(8,128)(2,1)} async-done(((bf16[512,2,768]{0,2,1:T(8,128)(2,1)}), bf16[512,2,192]{0,2,1:T(8,128)(2,1)}) %reduce-scatter.45.cloned.1.call-update) | async-done | bytes 393232 | tf_op jit(solution)/shard_map/reduce_scatter | solution.py:128
  1961.2 36.5 %reduce-scatter.43.cloned.1.call-done = bf16[512,2,192]{0,2,1:T(8,128)(2,1)} async-done(((bf16[512,2,768]{0,2,1:T(8,128)(2,1)}), bf16[512,2,192]{0,2,1:T(8,128)(2,1)}) %reduce-scatter.43.cloned.1.call-update) | async-done | bytes 393232 | tf_op jit(solution)/shard_map/reduce_scatter | solution.py:128
  2002.7 62.7 %reduce-scatter.77.cloned.1.call-done = bf16[384,1152]{1,0:T(8,128)(2,1)} async-done(((bf16[1536,1152]{1,0:T(8,128)(2,1)}), bf16[384,1152]{1,0:T(8,128)(2,1)}) %reduce-scatter.77.cloned.1.call-update) | async-done | bytes 884752
  2067.6 66.8 %reduce-scatter.75.cloned.1.call-done = bf16[384,1152]{1,0:T(8,128)(2,1)} async-done(((bf16[1536,1152]{1,0:T(8,128)(2,1)}), bf16[384,1152]{1,0:T(8,128)(2,1)}) %reduce-scatter.75.cloned.1.call-update) | async-done | bytes 884752
  2146.5 51.4 %reduce-scatter.41.cloned.1.call-done = bf16[2,192,2,512]{3,1,2,0:T(8,128)(2,1)} async-done(((bf16[2,768,2,512]{3,1,2,0:T(8,128)(2,1)}), bf16[2,192,2,512]{3,1,2,0:T(8,128)(2,1)}) %reduce-scatter.41.cloned.1.call-update) | async-done | bytes 786448 | tf_op jit(solution)/shard_map/reduce_scatter | solution.py:122
  2198.0 62.5 %reduce-scatter.39.cloned.1.call-done = bf16[2,192,2,512]{3,1,2,0:T(8,128)(2,1)} async-done(((bf16[2,768,2,512]{3,1,2,0:T(8,128)(2,1)}), bf16[2,192,2,512]{3,1,2,0:T(8,128)(2,1)}) %reduce-scatter.39.cloned.1.call-update) | async-done | bytes 786448 | tf_op jit(solution)/shard_map/reduce_scatter | solution.py:122
  2275.0 8.4 reduce-scatter.69.cloned.1.call-done
  2284.4 20.3 reduce-scatter.67.cloned.1.call-done
  2314.8 113.9 %reduce-scatter.65.cloned.1.call-done = bf16[384,2,1152]{2,0,1:T(8,128)(2,1)} async-done(((bf16[1536,2,1152]{2,0,1:T(8,128)(2,1)}), bf16[384,2,1152]{2,0,1:T(8,128)(2,1)}) %reduce-scatter.65.cloned.1.call-update) | async-done | bytes 1769488 | tf_op jit(solution)/shard_map/reduce_scatter | solution.py:131
  2428.6 126.4 %reduce-scatter.63.cloned.1.call-done = bf16[384,2,1152]{2,0,1:T(8,128)(2,1)} async-done(((bf16[1536,2,1152]{2,0,1:T(8,128)(2,1)}), bf16[384,2,1152]{2,0,1:T(8,128)(2,1)}) %reduce-scatter.63.cloned.1.call-update) | async-done | bytes 1769488 | tf_op jit(solution)/shard_map/reduce_scatter | solution.py:131
  2555.0 126.4 %reduce-scatter.61.cloned.1.call-done = bf16[384,2,1152]{2,0,1:T(8,128)(2,1)} async-done(((bf16[1536,2,1152]{2,0,1:T(8,128)(2,1)}), bf16[384,2,1152]{2,0,1:T(8,128)(2,1)}) %reduce-scatter.61.cloned.1.call-update) | async-done | bytes 1769488 | tf_op jit(solution)/shard_map/reduce_scatter | solution.py:131
  2681.4 126.2 %reduce-scatter.59.cloned.1.call-done = bf16[384,2,1152]{2,0,1:T(8,128)(2,1)} async-done(((bf16[1536,2,1152]{2,0,1:T(8,128)(2,1)}), bf16[384,2,1152]{2,0,1:T(8,128)(2,1)}) %reduce-scatter.59.cloned.1.call-update) | async-done | bytes 1769488 | tf_op jit(solution)/shard_map/reduce_scatter | solution.py:131
  (902 shorter events, 1010.9 us)
Async XLA Ops:
  7.2 393.6 %all-reduce.93.cloned.1.call-start = ((), (), s32[]{:S(2)}) async-start(), calls=%async_computation.22 | async-start | bytes 6291456 | tf_op jit(solution)/shard_map/psum | solution.py:62
  15.2 13.9 collective-permute-start
  314.4 191.8 %all-reduce.95.cloned.1.call-start = ((), (), s32[]{:S(2)}) async-start(), calls=%async_computation.23 | async-start | bytes 6291456 | tf_op jit(solution)/shard_map/psum | solution.py:62
  419.0 242.8 %all-reduce.97.cloned.1.call-start = ((), (), s32[]{:S(2)}) async-start(), calls=%async_computation.24 | async-start | bytes 6291456 | tf_op jit(solution)/shard_map/psum | solution.py:62
  419.1 96.2 %collective-permute-start.7 = (bf16[2,256]{1,0:T(2,128)(2,1)}, bf16[2,256]{1,0:T(2,128)(2,1)}, u32[]{:S(2)}, u32[]{:S(2)}) collective-permute-start(bf16[2,256]{1,0:T(2,128)(2,1)} %copy-done.118), channel_id=1, source_target_pairs={} | collective-permute-start | bytes 3080 | tf_op jit(solution)/shard_map/ppermute | solution.py:15
  420.3 95.6 %collective-permute-start.8 = (bf16[2,256]{1,0:T(2,128)(2,1)}, bf16[2,256]{1,0:T(2,128)(2,1)}, u32[]{:S(2)}, u32[]{:S(2)}) collective-permute-start(bf16[2,256]{1,0:T(2,128)(2,1)} %copy-done.118), channel_id=1, source_target_pairs={{0,12},{1,13},{2,14},{3,15},{16,28},{17,29},{18,30},{19,31}} | collective-permute-start | bytes 3080 | tf_op jit(solution)/shard_map/ppermute | solution.py:15
  426.1 90.5 %collective-permute-start.9 = (bf16[2,256]{1,0:T(2,128)(2,1)}, bf16[2,256]{1,0:T(2,128)(2,1)}, u32[]{:S(2)}, u32[]{:S(2)}) collective-permute-start(bf16[2,256]{1,0:T(2,128)(2,1)} %copy-done.118), channel_id=1, source_target_pairs={{0,8},{4,12},{1,9},{5,13},{2,10},{6,14},{3,11},{7,15},{16,24},{20,... | collective-permute-start | bytes 3080 | tf_op jit(solution)/shard_map/ppermute | solution.py:15
  427.9 89.3 %collective-permute-start.10 = (bf16[2,256]{1,0:T(2,128)(2,1)}, bf16[2,256]{1,0:T(2,128)(2,1)}, u32[]{:S(2)}, u32[]{:S(2)}) collective-permute-start(bf16[2,256]{1,0:T(2,128)(2,1)} %copy-done.118), channel_id=1, source_target_pairs={{0,4},{4,8},{8,12},{1,5},{5,9},{9,13},{2,6},{6,10},{10,14},{3,7},{... | collective-permute-start | bytes 3080 | tf_op jit(solution)/shard_map/ppermute | solution.py:15
  526.6 17.8 collective-permute-start.3
  527.9 17.4 collective-permute-start.4
  533.9 12.4 collective-permute-start.5
  535.9 12.9 collective-permute-start.6
  569.2 204.2 %all-reduce.99.cloned.1.call-start = ((), (), s32[]{:S(2)}) async-start(), calls=%async_computation.25 | async-start | bytes 6291456 | tf_op jit(solution)/shard_map/psum | solution.py:62
  686.2 255.4 %all-reduce.101.cloned.1.call-start = ((), (), s32[]{:S(2)}) async-start(), calls=%async_computation.26 | async-start | bytes 7340032 | tf_op jit(solution)/shard_map/psum | solution.py:62
  816.8 13.0 collective-permute-start.14
  818.1 21.6 collective-permute-start.13
  819.4 20.3 collective-permute-start.12
  843.0 214.1 %all-reduce.103.cloned.1.call-start = ((), (), s32[]{:S(2)}) async-start(), calls=%async_computation.27 | async-start | bytes 6291456 | tf_op jit(solution)/shard_map/psum | solution.py:62
  970.0 561.0 %all-reduce.105.cloned.1.call-start = ((), (), s32[]{:S(2)}) async-start(), calls=%async_computation.50 | async-start | bytes 12582912 | tf_op jit(solution)/shard_map/psum | solution.py:62
  1395.3 172.4 %reduce-scatter.49.cloned.1.call-start = ((), (), s32[]{:S(2)}) async-start(), calls=%async_computation.33 | async-start | bytes 1474560 | tf_op jit(solution)/shard_map/reduce_scatter | solution.py:122
  1405.0 188.0 %reduce-scatter.47.cloned.1.call-start = ((), (), s32[]{:S(2)}) async-start(), calls=%async_computation.32 | async-start | bytes 1474560 | tf_op jit(solution)/shard_map/reduce_scatter | solution.py:122
  1410.1 213.0 %reduce-scatter.57.cloned.1.call-start = ((), (), s32[]{:S(2)}) async-start(), calls=%async_computation.37 | async-start | bytes 1474560 | tf_op jit(solution)/shard_map/reduce_scatter | solution.py:128
  1420.0 233.3 %reduce-scatter.55.cloned.1.call-start = ((), (), s32[]{:S(2)}) async-start(), calls=%async_computation.36 | async-start | bytes 1474560 | tf_op jit(solution)/shard_map/reduce_scatter | solution.py:128
  1425.6 295.1 %reduce-scatter.81.cloned.1.call-start = ((), (), s32[]{:S(2)}) async-start(), calls=%async_computation.49 | async-start | bytes 4423680
  1435.7 354.0 %reduce-scatter.79.cloned.1.call-start = ((), (), s32[]{:S(2)}) async-start(), calls=%async_computation.48 | async-start | bytes 4423680
  1445.9 367.5 %reduce-scatter.73.cloned.1.call-start = ((), (), s32[]{:S(2)}) async-start(), calls=%async_computation.45 | async-start | bytes 491520
  1449.7 384.9 %reduce-scatter.71.cloned.1.call-start = ((), (), s32[]{:S(2)}) async-start(), calls=%async_computation.44 | async-start | bytes 491520
  1451.4 406.7 %reduce-scatter.53.cloned.1.call-start = ((), (), s32[]{:S(2)}) async-start(), calls=%async_computation.35 | async-start | bytes 983040 | tf_op jit(solution)/shard_map/reduce_scatter | solution.py:125
  1453.9 429.1 %reduce-scatter.51.cloned.1.call-start = ((), (), s32[]{:S(2)}) async-start(), calls=%async_computation.34 | async-start | bytes 983040 | tf_op jit(solution)/shard_map/reduce_scatter | solution.py:125
  1456.3 467.3 %all-reduce.107.cloned.1.call-start = ((), (), s32[]{:S(2)}) async-start(), calls=%async_computation.51 | async-start | bytes 1048576
  1472.8 488.5 %reduce-scatter.45.cloned.1.call-start = ((), (), s32[]{:S(2)}) async-start(), calls=%async_computation.31 | async-start | bytes 1966080 | tf_op jit(solution)/shard_map/reduce_scatter | solution.py:128
  1480.7 517.0 %reduce-scatter.43.cloned.1.call-start = ((), (), s32[]{:S(2)}) async-start(), calls=%async_computation.30 | async-start | bytes 1966080 | tf_op jit(solution)/shard_map/reduce_scatter | solution.py:128
  1486.1 579.4 %reduce-scatter.77.cloned.1.call-start = ((), (), s32[]{:S(2)}) async-start(), calls=%async_computation.47 | async-start | bytes 4423680
  1496.2 638.3 %reduce-scatter.75.cloned.1.call-start = ((), (), s32[]{:S(2)}) async-start(), calls=%async_computation.46 | async-start | bytes 4423680
  1506.6 691.4 %reduce-scatter.41.cloned.1.call-start = ((), (), s32[]{:S(2)}) async-start(), calls=%async_computation.29 | async-start | bytes 3932160 | tf_op jit(solution)/shard_map/reduce_scatter | solution.py:122
  1515.6 744.8 %reduce-scatter.39.cloned.1.call-start = ((), (), s32[]{:S(2)}) async-start(), calls=%async_computation.28 | async-start | bytes 3932160 | tf_op jit(solution)/shard_map/reduce_scatter | solution.py:122
  1522.3 761.1 %reduce-scatter.69.cloned.1.call-start = ((), (), s32[]{:S(2)}) async-start(), calls=%async_computation.43 | async-start | bytes 491520
  1537.3 767.4 %reduce-scatter.67.cloned.1.call-start = ((), (), s32[]{:S(2)}) async-start(), calls=%async_computation.42 | async-start | bytes 491520
  1539.0 889.6 %reduce-scatter.65.cloned.1.call-start = ((), (), s32[]{:S(2)}) async-start(), calls=%async_computation.41 | async-start | bytes 8847360 | tf_op jit(solution)/shard_map/reduce_scatter | solution.py:131
  1545.6 1009.4 %reduce-scatter.63.cloned.1.call-start = ((), (), s32[]{:S(2)}) async-start(), calls=%async_computation.40 | async-start | bytes 8847360 | tf_op jit(solution)/shard_map/reduce_scatter | solution.py:131
  1552.1 1129.3 %reduce-scatter.61.cloned.1.call-start = ((), (), s32[]{:S(2)}) async-start(), calls=%async_computation.39 | async-start | bytes 8847360 | tf_op jit(solution)/shard_map/reduce_scatter | solution.py:131
  1558.6 1249.0 %reduce-scatter.59.cloned.1.call-start = ((), (), s32[]{:S(2)}) async-start(), calls=%async_computation.38 | async-start | bytes 8847360 | tf_op jit(solution)/shard_map/reduce_scatter | solution.py:131
  1595.6 60.4 %collective-permute-start.23 = (bf16[192,384]{1,0:T(8,128)(2,1)}, bf16[192,384]{1,0:T(8,128)(2,1)}, u32[]{:S(2)}, u32[]{:S(2)}) collective-permute-start(bf16[192,384]{1,0:T(8,128)(2,1)} %fusion.226), channel_id=1, source_target_pairs={{16,0},{17,1},{18,2},{19,3},{20,4},{21,5},{22,6},{23,7},{24,8},{25... | collective-permute-start | bytes 442376 | tf_op jit(solution)/shard_map/ppermute | solution.py:15
  1885.4 24.0 collective-permute-start.24
  1925.8 74.5 %collective-permute-start.20 = (bf16[4,16,2,128]{3,0,2,1:T(4,128)(2,1)}, bf16[4,16,2,128]{3,0,2,1:T(4,128)(2,1)}, u32[]{:S(2)}, u32[]{:S(2)}) collective-permute-start(bf16[4,16,2,128]{3,0,2,1:T(4,128)(2,1)} %fusion.237), channel_id=1, source_target_pairs={{0,16},{1,17},{2,18},{3,19},{4,20},{5,21},{6,22},{7,23},{8,24},{9,... | collective-permute-start | bytes 98312 | tf_op jit(solution)/shard_map/ppermute | solution.py:15
  2145.2 164.7 %collective-permute-start.11 = (bf16[256,1536]{1,0:T(8,128)(2,1)}, bf16[256,1536]{1,0:T(8,128)(2,1)}, u32[]{:S(2)}, u32[]{:S(2)}) collective-permute-start(bf16[256,1536]{1,0:T(8,128)(2,1)} %slice_bitcast_fusion.42), channel_id=1, source_target_pairs={{16,0},{17,1},{18,2},{19,3},{20,4},{21,5},{22,6},{23,7},{24,8},{25... | collective-permute-start | bytes 2359304 | tf_op jit(solution)/shard_map/ppermute | solution.py:15
  2263.2 43.9 %collective-permute-start.19 = (bf16[192,2,512]{2,0,1:T(8,128)(2,1)}, bf16[192,2,512]{2,0,1:T(8,128)(2,1)}, u32[]{:S(2)}, u32[]{:S(2)}) collective-permute-start(bf16[192,2,512]{2,0,1:T(8,128)(2,1)} %fusion.202), channel_id=1, source_target_pairs={{0,16},{1,17},{2,18},{3,19},{4,20},{5,21},{6,22},{7,23},{8,24},{9,... | collective-permute-start | bytes 1179656 | tf_op jit(solution)/shard_map/ppermute | solution.py:15
  2272.8 39.4 %collective-permute-start.18 = (bf16[256,1536]{1,0:T(8,128)(2,1)}, bf16[256,1536]{1,0:T(8,128)(2,1)}, u32[]{:S(2)}, u32[]{:S(2)}) collective-permute-start(bf16[256,1536]{1,0:T(8,128)(2,1)} %fusion.172), channel_id=1, source_target_pairs={{0,16},{1,17},{2,18},{3,19},{4,20},{5,21},{6,22},{7,23},{8,24},{9,... | collective-permute-start | bytes 2359304 | tf_op jit(solution)/shard_map/ppermute | solution.py:15
  (147 other events, 973.8 us)
Sparse Core Ops, SparseCore 0:
  314.5 86.2 all-reduce.92
  419.2 86.9 all-reduce.94
  569.3 92.5 all-reduce.96
  686.3 86.9 all-reduce.98
  843.1 98.4 all-reduce.100
  970.2 86.9 all-reduce.102
  1395.4 135.5 all-reduce.104
  1533.3 29.3 reduce-scatter.48
  1565.0 27.9 reduce-scatter.46
  1595.1 27.9 reduce-scatter.56
  1625.4 27.9 reduce-scatter.54
  1655.5 65.0 reduce-scatter.80
  1723.0 66.6 reduce-scatter.78
  1792.4 20.9 reduce-scatter.72
  1815.5 19.0 reduce-scatter.70
  1836.7 21.3 reduce-scatter.52
  1860.3 22.6 reduce-scatter.50
  1885.2 38.3 all-reduce.106
  1925.9 35.2 reduce-scatter.44
  1963.4 34.2 reduce-scatter.42
  2000.0 65.3 reduce-scatter.76
  2067.7 66.6 reduce-scatter.74
  2137.4 60.5 reduce-scatter.40
  2200.1 60.2 reduce-scatter.38
  2262.7 20.6 reduce-scatter.68
  2285.6 19.0 reduce-scatter.66
  2306.8 121.7 reduce-scatter.64
  2430.9 124.0 reduce-scatter.62
  2557.3 124.0 reduce-scatter.60
  2683.5 124.0 reduce-scatter.58
where the time goes:
time: 2850 us; the launch traced here: 2820 us
  waiting for transfers between devices  1670 us (59%)
  local copies, waits for them, and re-layouts  550 us (19%)
  other arithmetic  287 us (10%)
  matrix products  167 us (6%)
  blocking collectives  75.1 us (3%)
  starting transfers between devices  59.4 us (2%)
    psum x7, waiting for transfers between devices, head_total(): return lax.psum(partial_value, 'head')  495 us
    reduce_scatter x4, waiting for transfers between devices, seq_sum(): lax.psum_scatter(parts[3].astype(jnp.bfloat16), 'seq', scatter_dimension=...  493 us
    unnamed x39, waiting for transfers between devices  340 us
    reduce_scatter x4, waiting for transfers between devices, seq_sum(): lax.psum_scatter(parts[0].astype(jnp.bfloat16), 'seq', scatter_dimension=...  139 us
    reduce_scatter x4, waiting for transfers between devices, seq_sum(): lax.psum_scatter(parts[2].astype(jnp.bfloat16), 'seq', scatter_dimension=...  126 us
    slice x57, local copies, waits for them, and re-layouts, rec_backward(): lax.associative_scan(affine, (following, grad_hidden), reverse=True, axis=1)  120 us
    slice x52, local copies, waits for them, and re-layouts, rec_forward(): through, local_state = lax.associative_scan(affine, (decays, drive), axis=1)  92.4 us
    unnamed x262, local copies, waits for them, and re-layouts  80.3 us
  transfers between devices with their start and end apart: 56, of which 34 were waited for; matrix products, arithmetic and copies ran while one was open for 10% of the time, Pallas kernels for 0%

commit v1 on v0

v1 whole, which is shorter than its diff:
```python
import functools

import jax
import jax.numpy as jnp
from jax import lax
from jax.experimental import pallas as pl
from jax.experimental.pallas import tpu as pltpu
from jax.sharding import PartitionSpec as P

WINDOW = 1024
EPSILON = 1e-06
MESH = pl.DeviceIdType.MESH
F32 = jnp.float32
BF16 = jnp.bfloat16
SWAP = [(0, 1), (1, 0)]


def dot(a, b, dims, out=F32):
    return lax.dot_general(a, b, ((dims[:1], dims[1:]), ((), ())), preferred_element_type=F32).astype(
        out
    )


def vmem():
    return pl.BlockSpec(memory_space=pltpu.VMEM)


def meet(axis, me, n):
    barrier = pltpu.get_barrier_semaphore()
    for k in range(1, n):
        peer = lax.rem(me + k, n)
        pl.semaphore_signal(barrier, inc=1, device_id={axis: peer}, device_id_type=MESH)
    pl.semaphore_wait(barrier, n - 1)


def remote(src, dst, send, recv, axis, peer):
    return pltpu.make_async_remote_copy(
        src_ref=src,
        dst_ref=dst,
        send_sem=send,
        recv_sem=recv,
        device_id={axis: peer},
        device_id_type=MESH,
    )


def scatter_sum(n, me, rows, part, recv, send_sem, recv_sem):
    copies = []
    for k in range(1, n):
        peer = lax.rem(me + k, n)
        start = pl.multiple_of(peer * rows, rows)
        copies.append(
            remote(
                part.at[pl.ds(start, rows)],
                recv.at[k - 1],
                send_sem.at[k - 1],
                recv_sem.at[k - 1],
                "head",
                peer,
            )
        )
    for copy in copies:
        copy.start()
    total = part[pl.ds(pl.multiple_of(me * rows, rows), rows)].astype(F32)
    for k, copy in enumerate(copies):
        copy.wait_recv()
        total = total + recv[k].astype(F32)
    for copy in copies:
        copy.wait_send()
    return total


def spread(n, me, rows, value, full, send_sem, recv_sem):
    mine = pl.ds(pl.multiple_of(me * rows, rows), rows)
    full[mine] = value
    copies = []
    for k in range(1, n):
        peer = lax.rem(me + k, n)
        copies.append(
            remote(
                full.at[mine], full.at[mine], send_sem.at[k - 1], recv_sem.at[k - 1], "head", peer
            )
        )
    for copy in copies:
        copy.start()
    for copy in copies:
        copy.wait()


def forward_body(n, kind, part, base, gain, new, full, recv, s1, r1, s2, r2):
    me = lax.axis_index("head")
    rows = base.shape[0]
    meet("head", me, n)
    fresh = base[...] + scatter_sum(n, me, rows, part, recv, s1, r1)
    if kind == "last":
        new[...] = fresh
        out = fresh
    else:
        if kind == "round":
            fresh = fresh.astype(BF16).astype(F32)
        new[...] = fresh
        out = fresh * lax.rsqrt(jnp.mean(fresh * fresh, axis=-1, keepdims=True) + EPSILON)
        out = out * gain[...]
    spread(n, me, rows, out.astype(BF16), full, s2, r2)


def backward_body(n, kind, part, base, gain, up, res, gain_grad, full, recv, s1, r1, s2, r2):
    me = lax.axis_index("head")
    rows = base.shape[0]
    meet("head", me, n)
    grad = scatter_sum(n, me, rows, part, recv, s1, r1)
    v = base[...]
    scale = lax.rsqrt(jnp.mean(v * v, axis=-1, keepdims=True) + EPSILON)
    gain_grad[...] = jnp.sum(grad * v * scale, axis=0, keepdims=True)
    inner = grad * gain[...]
    out = up[...] + scale * inner - v * (
        scale * scale * scale * jnp.mean(inner * v, axis=-1, keepdims=True)
    )
    if kind == "round":
        out = out.astype(BF16).astype(F32)
    res[...] = out
    spread(n, me, rows, out.astype(BF16), full, s2, r2)


def boundary_scratch(n, rows, width):
    return [pltpu.VMEM((n - 1, rows, width), BF16)] + [pltpu.SemaphoreType.DMA((n - 1,))] * 4


def join_forward(kind, part, base, gain, ident):
    n = lax.axis_size("head")
    count, width = part.shape
    rows = base.shape[0]
    return pl.pallas_call(
        functools.partial(forward_body, n, kind),
        name=f"join_forward_{ident}",
        out_shape=(
            jax.ShapeDtypeStruct((rows, width), F32),
            jax.ShapeDtypeStruct((count, width), BF16),
        ),
        in_specs=[vmem()] * 3,
        out_specs=(vmem(), vmem()),
        scratch_shapes=boundary_scratch(n, rows, width),
        compiler_params=pltpu.CompilerParams(collective_id=ident, has_side_effects=True),
    )(part, base, gain)


def join_backward(kind, part, base, gain, up, ident):
    n = lax.axis_size("head")
    count, width = part.shape
    rows = base.shape[0]
    return pl.pallas_call(
        functools.partial(backward_body, n, kind),
        name=f"join_backward_{ident}",
        out_shape=(
            jax.ShapeDtypeStruct((rows, width), F32),
            jax.ShapeDtypeStruct((1, width), F32),
            jax.ShapeDtypeStruct((count, width), BF16),
        ),
        in_specs=[vmem()] * 4,
        out_specs=(vmem(), vmem(), vmem()),
        scratch_shapes=boundary_scratch(n, rows, width),
        compiler_params=pltpu.CompilerParams(collective_id=ident, has_side_effects=True),
    )(part, base, gain, up)


def carry_body(n, reverse, edge, out, every, send_sem, recv_sem):
    me = lax.axis_index("seq")
    meet("seq", me, n)
    copies = []
    for k in range(1, n):
        peer = lax.rem(me + k, n)
        copies.append(
            remote(edge, every.at[k - 1], send_sem.at[k - 1], recv_sem.at[k - 1], "seq", peer)
        )
    for copy in copies:
        copy.start()
    for copy in copies:
        copy.wait()
    state = jnp.zeros((1, edge.shape[1]), F32)
    order = range(1, n) if reverse else range(n - 1, 0, -1)
    for k in order:
        sender = me - k if not reverse else me + n - k
        inside = sender >= 0 if not reverse else sender < n
        if reverse:
            inside = jnp.logical_and(inside, sender > me)
        slot = every[k - 1]
        state = jnp.where(inside, slot[0:1] * state + slot[1:2], state)
    out[...] = jnp.broadcast_to(state, out.shape)


def carry(edge, reverse, ident):
    n = lax.axis_size("seq")
    return pl.pallas_call(
        functools.partial(carry_body, n, reverse),
        name=f"carry_{ident}",
        out_shape=jax.ShapeDtypeStruct(edge.shape, F32),
        in_specs=[vmem()],
        out_specs=vmem(),
        scratch_shapes=[
            pltpu.VMEM((n - 1,) + edge.shape, F32),
            pltpu.SemaphoreType.DMA((n - 1,)),
            pltpu.SemaphoreType.DMA((n - 1,)),
        ],
        compiler_params=pltpu.CompilerParams(collective_id=ident, has_side_effects=True),
    )(edge)


def shifted(x, by, row, fill):
    count = x.shape[0]
    if by > 0:
        return jnp.where(row >= by, pltpu.roll(x, by, 0), fill)
    return jnp.where(row < count + by, pltpu.roll(x, count + by, 0), fill)


def scan_rows(a, b, row, sign):
    step = 1
    while step < a.shape[0]:
        b = b + a * shifted(b, sign * step, row, 0.0)
        a = a * shifted(a, sign * step, row, 1.0)
        step *= 2
    return a, b


def minus_expm1(y):
    series = jnp.full_like(y, 1.0)
    for k in range(9, 1, -1):
        series = 1.0 + y * series * (1.0 / k)
    return jnp.where(y > -0.5, -y * series, 1.0 - jnp.exp(y))


def gelu_parts(x):
    c = 0.7978845608028654
    inner = c * (x + 0.044715 * x * x * x)
    t = jnp.tanh(inner)
    act = 0.5 * x * (1.0 + t)
    slope = 0.5 * (1.0 + t) + 0.5 * x * (1.0 - t * t) * c * (1.0 + 3.0 * 0.044715 * x * x)
    return act, slope


def rec_forward_body(ext, masks, chan, soft, gates, conv_out, pre_out, through, local, edge):
    count = conv_out.shape[0]
    block = conv_out.shape[1]
    wide = ext[...].astype(F32)
    total = chan[4:5] + chan[0:1] * wide[8:]
    for k in range(1, 4):
        total = total + chan[k : k + 1] * pltpu.roll(wide, k, 0)[8:] * masks[:, k : k + 1]
    low = total.astype(BF16)
    conv_out[...] = low
    pre = jnp.dot(low, gates[0], preferred_element_type=F32)
    rate = pre[:, :block] + chan[5:6]
    gate = pre[:, block:] + chan[6:7]
    pre_out[0] = rate
    pre_out[1] = gate
    log_decay = -8.0 * jax.nn.sigmoid(rate) * soft[0:1]
    decay = jnp.exp(log_decay) * masks[:, 1:2]
    drive = jnp.sqrt(minus_expm1(2.0 * log_decay)) * jax.nn.sigmoid(gate) * low.astype(F32)
    row = lax.broadcasted_iota(jnp.int32, (count, block), 0)
    a, b = scan_rows(decay, drive, row, 1)
    through[...] = a
    local[...] = b
    edge[0:1] = a[count - 1 :]
    edge[1:2] = b[count - 1 :]
    edge[2:8] = jnp.zeros((6, block), F32)


def rec_forward_local(ext, masks, chan, soft, gates):
    count, chans = ext.shape[0] - 8, ext.shape[1]
    blocks, block = gates.shape[:2]
    wide = pl.BlockSpec((count, block), lambda i: (0, i))
    row8 = pl.BlockSpec((8, block), lambda i: (0, i))
    return pl.pallas_call(
        rec_forward_body,
        name="rec_forward_local",
        grid=(blocks,),
        out_shape=(
            jax.ShapeDtypeStruct((count, chans), BF16),
            jax.ShapeDtypeStruct((2, count, chans), F32),
            jax.ShapeDtypeStruct((count, chans), F32),
            jax.ShapeDtypeStruct((count, chans), F32),
            jax.ShapeDtypeStruct((8, chans), F32),
        ),
        in_specs=[
            pl.BlockSpec((count + 8, block), lambda i: (0, i)),
            pl.BlockSpec((count, 4), lambda i: (0, 0)),
            row8,
            row8,
            pl.BlockSpec((1, block, 2 * block), lambda i: (i, 0, 0)),
        ],
        out_specs=(
            wide,
            pl.BlockSpec((2, count, block), lambda i: (0, 0, i)),
            wide,
            wide,
            row8,
        ),
    )(ext, masks, chan, soft, gates)


def rec_back_first_body(gm, gate_pre, hidden, rate, soft, masks, grad_gate, beyond, local, edge):
    count, block = gm.shape
    act, slope = gelu_parts(gate_pre[...])
    up = gm[...]
    grad_gate[...] = (up * hidden[...] * slope).astype(BF16)
    decay = jnp.exp(-8.0 * jax.nn.sigmoid(rate[0]) * soft[0:1]) * masks[:, 1:2]
    row = lax.broadcasted_iota(jnp.int32, (count, block), 0)
    a, b = scan_rows(shifted(decay, -1, row, 1.0), up * act, row, -1)
    beyond[...] = a
    local[...] = b
    edge[0:1] = decay[0:1] * a[0:1]
    edge[1:2] = decay[0:1] * b[0:1]
    edge[2:8] = jnp.zeros((6, block), F32)


def rec_back_first(gm, gate_pre, hidden, pre, soft, masks, block):
    count, chans = gm.shape
    wide = pl.BlockSpec((count, block), lambda i: (0, i))
    row8 = pl.BlockSpec((8, block), lambda i: (0, i))
    return pl.pallas_call(
        rec_back_first_body,
        name="rec_back_first",
        grid=(chans // block,),
        out_shape=(
            jax.ShapeDtypeStruct((count, chans), BF16),
            jax.ShapeDtypeStruct((count, chans), F32),
            jax.ShapeDtypeStruct((count, chans), F32),
            jax.ShapeDtypeStruct((8, chans), F32),
        ),
        in_specs=[
            wide,
            wide,
            wide,
            pl.BlockSpec((1, count, block), lambda i: (0, 0, i)),
            row8,
            pl.BlockSpec((count, 4), lambda i: (0, 0)),
        ],
        out_specs=(wide, wide, wide, row8),
    )(gm, gate_pre, hidden, pre, soft, masks)


def rec_back_second_body(
    beyond, local, arriving, hidden, entering, pre, conv, chan, soft, gates, masks, ext,
    gate_low, grad_values, edge, chan_grad,
):
    count, block = local.shape
    row = lax.broadcasted_iota(jnp.int32, (count, block), 0)
    state = local[...] + beyond[...] * arriving[0:1]
    earlier = jnp.where(row >= 1, pltpu.roll(hidden[...], 1, 0), entering[0:1])
    low = conv[...].astype(F32)
    keep_rate = jax.nn.sigmoid(pre[0])
    log_decay = -8.0 * keep_rate * soft[0:1]
    decay = jnp.exp(log_decay)
    size = jnp.sqrt(minus_expm1(2.0 * log_decay))
    gate = jax.nn.sigmoid(pre[1])
    grad_decay = state * earlier * masks[:, 1:2]
    grad_log = grad_decay * decay - state * gate * low * (decay * decay / size)
    grad_rate = grad_log * (-8.0 * soft[0:1]) * keep_rate * (1.0 - keep_rate)
    grad_gate = state * size * low * gate * (1.0 - gate)
    rate_low = grad_rate.astype(BF16)
    gate_low_part = grad_gate.astype(BF16)
    gate_low[0] = rate_low
    gate_low[1] = gate_low_part
    weights = gates[0]
    over = (((1,), (1,)), ((), ()))
    grad_conv = (
        state * size * gate
        + lax.dot_general(rate_low, weights[:, :block], over, preferred_element_type=F32)
        + lax.dot_general(gate_low_part, weights[:, block:], over, preferred_element_type=F32)
    )
    wide = ext[...].astype(F32)
    total = chan[0:1] * grad_conv
    chan_grad[0:1] = jnp.sum(grad_conv * wide[8:], axis=0, keepdims=True)
    row8 = lax.broadcasted_iota(jnp.int32, (8, block), 0)
    over_edge = jnp.zeros((8, block), F32)
    for k in range(1, 4):
        masked = grad_conv * masks[:, k : k + 1]
        chan_grad[k : k + 1] = jnp.sum(masked * pltpu.roll(wide, k, 0)[8:], axis=0, keepdims=True)
        back = chan[k : k + 1] * masked
        total = total + shifted(back, -k, row, 0.0)
        first = back[0:8]
        if k < 3:
            first = pltpu.roll(first, 3 - k, 0)
        over_edge = over_edge + jnp.where((row8 >= 3 - k) & (row8 < 3), first, 0.0)
    grad_values[...] = total
    edge[...] = over_edge
    chan_grad[4:5] = jnp.sum(grad_conv, axis=0, keepdims=True)
    chan_grad[5:6] = jnp.sum(grad_rate, axis=0, keepdims=True)
    chan_grad[6:7] = jnp.sum(grad_gate, axis=0, keepdims=True)
    chan_grad[7:8] = jnp.sum(grad_log * keep_rate, axis=0, keepdims=True) * (
        -8.0 * jax.nn.sigmoid(chan[7:8])
    )


def rec_back_second(beyond, local, arriving, hidden, entering, pre, conv, chan, soft, gates, masks, ext):
    count, chans = local.shape
    blocks, block = gates.shape[:2]
    wide = pl.BlockSpec((count, block), lambda i: (0, i))
    row8 = pl.BlockSpec((8, block), lambda i: (0, i))
    pair = pl.BlockSpec((2, count, block), lambda i: (0, 0, i))
    return pl.pallas_call(
        rec_back_second_body,
        name="rec_back_second",
        grid=(blocks,),
        out_shape=(
            jax.ShapeDtypeStruct((2, count, chans), BF16),
            jax.ShapeDtypeStruct((count, chans), F32),
            jax.ShapeDtypeStruct((8, chans), F32),
            jax.ShapeDtypeStruct((8, chans), F32),
        ),
        in_specs=[
            wide,
            wide,
            row8,
            wide,
            row8,
            pair,
            wide,
            row8,
            row8,
            pl.BlockSpec((1, block, 2 * block), lambda i: (i, 0, 0)),
            pl.BlockSpec((count, 4), lambda i: (0, 0)),
            pl.BlockSpec((count + 8, block), lambda i: (0, i)),
        ],
        out_specs=(pair, wide, row8, row8),
    )(beyond, local, arriving, hidden, entering, pre, conv, chan, soft, gates, masks, ext)


def from_behind(array, axis, by):
    devices = lax.axis_size(axis)
    pairs = [(i, i + by) for i in range(devices) if 0 <= i + by < devices]
    return lax.ppermute(array, axis, pairs)


def swapped(array):
    return lax.ppermute(array, "section", SWAP)


def attend(query_rows, key_rows, allowed):
    head_dim = query_rows.shape[2]
    scores = jnp.einsum(
        "qhd,kd->hqk", query_rows, key_rows[:, :head_dim], preferred_element_type=F32
    ) * head_dim ** (-0.5)
    masked = jnp.where(allowed[None], scores, -1e30)
    row_max = jnp.max(masked, axis=-1, keepdims=True)
    lifted = jnp.exp(masked - row_max)
    row_total = jnp.sum(lifted, axis=-1, keepdims=True)
    weights = (lifted / row_total).astype(BF16)
    attended = jnp.einsum(
        "hqk,kd->qhd", weights, key_rows[:, head_dim:], preferred_element_type=F32
    ).astype(BF16)
    return (attended, row_max[:, :, 0] + jnp.log(row_total[:, :, 0]))


def attend_back(query_rows, key_rows, allowed, log_total, grad_rows):
    head_dim = query_rows.shape[2]
    factor = head_dim ** (-0.5)
    scores = (
        jnp.einsum("qhd,kd->hqk", query_rows, key_rows[:, :head_dim], preferred_element_type=F32)
        * factor
    )
    probs = jnp.exp(jnp.where(allowed[None], scores, -1e30) - log_total[:, :, None])
    weights = probs.astype(BF16)
    grad_probs = jnp.einsum(
        "qhd,kd->hqk", grad_rows, key_rows[:, head_dim:], preferred_element_type=F32
    )
    grad_values = jnp.einsum("hqk,qhd->kd", weights, grad_rows, preferred_element_type=F32)
    grad_scores = (
        probs * (grad_probs - jnp.sum(grad_probs * probs, axis=-1, keepdims=True))
    ).astype(BF16)
    grad_query = (
        jnp.einsum("hqk,kd->qhd", grad_scores, key_rows[:, :head_dim], preferred_element_type=F32)
        * factor
    )
    grad_keys = (
        jnp.einsum("hqk,qhd->kd", grad_scores, query_rows, preferred_element_type=F32) * factor
    )
    return (grad_query, jnp.concatenate([grad_keys, grad_values], axis=-1))


def mlp_forward(normed, w_in, w_out):
    gate_up = jnp.einsum("td,dkf->tkf", normed, w_in, preferred_element_type=F32)
    hidden = (jax.nn.gelu(gate_up[:, 0]) * gate_up[:, 1]).astype(BF16)
    return gate_up, hidden, dot(hidden, w_out, (1, 0), BF16)


def mlp_backward(gate_up, w_in, w_out, out_low):
    grad_hidden = dot(out_low, w_out, (1, 1))
    act, slope = gelu_parts(gate_up[:, 0])
    grad_gate = (grad_hidden * gate_up[:, 1] * slope).astype(BF16)
    grad_up = (grad_hidden * act).astype(BF16)
    part = (
        dot(grad_gate, w_in[:, 0], (1, 1)) + dot(grad_up, w_in[:, 1], (1, 1))
    ).astype(BF16)
    return grad_gate, grad_up, part


def seq_scatter(grad):
    return lax.psum_scatter(grad, "seq", scatter_dimension=0, tiled=True)


def pair_grad(left, left_other, right, right_other):
    return (dot(left, right, (0, 0)) + dot(left_other, right_other, (0, 0))).astype(BF16)


def columns(array, start, size):
    return lax.dynamic_slice_in_dim(array, start, size, axis=1)


def on_device(
    inputs,
    segments,
    norms,
    rec_in,
    rec_gates,
    rec_chan,
    rec_out,
    attn_q,
    attn_kv,
    attn_out,
    mlp_in,
    mlp_out,
    cotangent,
):
    core = lax.axis_index("section")
    first = core == 0
    place = lax.axis_index("seq")
    rank = lax.axis_index("head")
    heads = lax.axis_size("head")
    blocks_seq = lax.axis_size("seq")
    _, count, width = inputs.shape
    rows = count // heads
    chans = rec_in.shape[2]
    blocks, block = rec_gates.shape[:2]
    half_width = width // 2

    def pick(array, index):
        return lax.dynamic_index_in_dim(array, index, 0, keepdims=False)

    def own_rows(array):
        return lax.dynamic_slice_in_dim(array, rank * rows, rows, axis=0)

    def mine_and_other(pair_zero, pair_one):
        return jnp.where(first, pair_zero, pair_one), swapped(jnp.where(first, pair_one, pair_zero))

    other_in, other_out, other_norms = swapped(mlp_in[0]), swapped(mlp_out[0]), swapped(norms[0])
    gains = [
        jnp.where(first, norms[0], other_norms),
        jnp.where(first, other_norms, norms[0]),
    ]
    gain = [[gains[l][k][None] for k in range(2)] for l in range(2)]
    w_in = [jnp.where(first, mlp_in[0], other_in), jnp.where(first, other_in, mlp_in[0])]
    w_out = [jnp.where(first, mlp_out[0], other_out), jnp.where(first, other_out, mlp_out[0])]

    stream_low = pick(inputs, core)
    stream = stream_low.astype(F32)
    top_low = pick(cotangent, core)
    ids = pick(segments, core)
    every_id = lax.all_gather(ids, "seq")

    def rooted(x):
        return x * lax.rsqrt(jnp.mean(x * x, axis=-1, keepdims=True) + EPSILON) * gain[0][0]

    normed_one = rooted(stream).astype(BF16)
    branches = jnp.einsum("td,dkr->ktr", normed_one, rec_in, preferred_element_type=F32)
    values = branches[0].astype(BF16)
    gate_pre = branches[1]
    before = from_behind(values[-8:], "seq", 1)
    ext = jnp.concatenate([before, values], axis=0)
    before_ids = pick(every_id, jnp.maximum(place - 1, 0))[-3:]
    ext_ids = jnp.concatenate([jnp.where(place == 0, -1, before_ids), ids])
    masks = jnp.stack(
        [(ext_ids[3 - k : 3 - k + count] == ids).astype(F32) for k in range(4)], axis=1
    )
    soft = jnp.broadcast_to(jax.nn.softplus(rec_chan[7:8]), rec_chan.shape)
    gates_flat = rec_gates.reshape(blocks, block, 2 * block)
    conv_low, pre, through, local, edge = rec_forward_local(ext, masks, rec_chan, soft, gates_flat)
    entering = carry(edge, False, 0)
    hidden_state = local + through * entering[0:1]
    mixed = (hidden_state * jax.nn.gelu(gate_pre)).astype(BF16)
    part = dot(mixed, rec_out, (1, 0), BF16)
    res_one, normed_a = join_forward("keep", part, own_rows(stream), gain[0][1], 1)

    gate_up_a, hidden_a, part = mlp_forward(normed_a, w_in[0], w_out[0])
    passed, normed_two = join_forward("round", part, res_one, gain[1][0], 2)

    head_dim = attn_kv.shape[1] // 2
    heads_here = attn_q.shape[1] // head_dim
    queries = dot(normed_two, attn_q, (1, 0), BF16).reshape(count, heads_here, head_dim)
    keyval = dot(normed_two, attn_kv, (1, 0), BF16)
    reach = min(max(1, WINDOW // count), blocks_seq - 1)
    window_kv = [from_behind(keyval, "seq", distance) for distance in range(reach, 0, -1)]
    all_keys = jnp.concatenate(window_kv + [keyval], axis=0)
    key_ids = jnp.concatenate(
        [pick(every_id, jnp.maximum(place - distance, 0)) for distance in range(reach, 0, -1)]
        + [ids]
    )
    key_spots = (place - reach) * count + jnp.arange((reach + 1) * count, dtype=jnp.int32)
    query_spots = place * count + jnp.arange(count, dtype=jnp.int32)
    distance_q = query_spots[:, None] - key_spots[None, :]
    inside = (distance_q >= 0) & (distance_q < WINDOW) & (key_spots >= 0)[None, :]
    allowed = inside & (ids[:, None] == key_ids[None, :])
    attended, log_totals = attend(queries, all_keys, allowed)
    attended = attended.reshape(count, heads_here * head_dim)
    part = dot(attended, attn_out, (1, 0), BF16)
    res_two, normed_b = join_forward("keep", part, passed, gain[1][1], 3)

    gate_up_b, hidden_b, part = mlp_forward(normed_b, w_in[1], w_out[1])
    _, final = join_forward("last", part, res_two, gain[1][1], 4)

    def mlp_grads(normed, hidden, grad_gate, grad_up, out_low, out_other):
        side, side_other = mine_and_other(grad_gate, grad_up)
        units = hidden.shape[1] // 2
        kept = columns(hidden, core * units, units)
        kept_other = swapped(columns(hidden, (1 - core) * units, units))
        grad_in = pair_grad(normed, swapped(normed), side, side_other)
        grad_out = pair_grad(out_low, out_other, kept, kept_other)
        return seq_scatter(grad_in), seq_scatter(grad_out)

    def half_columns(array):
        own = columns(array, core * half_width, half_width)
        return own, swapped(columns(array, (1 - core) * half_width, half_width))

    def half_grad(array_pair, right):
        return seq_scatter(pair_grad(array_pair[0], array_pair[1], right, swapped(right)))

    grad_gate_b, grad_up_b, part = mlp_backward(gate_up_b, w_in[1], w_out[1], top_low)
    grads_b = mlp_grads(
        normed_b, hidden_b, grad_gate_b, grad_up_b, top_low, pick(cotangent, 1 - core)
    )
    grad_res_two, gain_b, low_two = join_backward(
        "keep", part, res_two, gain[1][1], own_rows(top_low.astype(F32)), 5
    )

    grad_att = dot(low_two, attn_out, (1, 1), BF16)
    grad_query, grad_kv = attend_back(
        queries, all_keys, allowed, log_totals, grad_att.reshape(count, heads_here, head_dim)
    )
    own_kv = grad_kv[reach * count :]
    for distance in range(1, reach + 1):
        start = (reach - distance) * count
        own_kv = own_kv + from_behind(
            grad_kv[start : start + count].astype(BF16), "seq", -distance
        ).astype(F32)
    query_low = grad_query.reshape(count, heads_here * head_dim).astype(BF16)
    kv_part = own_kv.astype(BF16)
    part = (dot(query_low, attn_q, (1, 1)) + dot(kv_part, attn_kv, (1, 1))).astype(BF16)
    grad_passed, gain_two, low_passed = join_backward(
        "round", part, passed, gain[1][0], grad_res_two, 6
    )
    kv_low = lax.psum(kv_part.astype(F32), "head").astype(BF16)

    grad_gate_a, grad_up_a, part = mlp_backward(gate_up_a, w_in[0], w_out[0], low_passed)
    grads_a = mlp_grads(
        normed_a, hidden_a, grad_gate_a, grad_up_a, low_passed, swapped(low_passed)
    )
    grad_res_one, gain_a, mix_low = join_backward(
        "keep", part, res_one, gain[0][1], grad_passed, 7
    )

    grad_mixed = dot(mix_low, rec_out, (1, 1))
    grad_branch, beyond, local_grad, edge = rec_back_first(
        grad_mixed, gate_pre, hidden_state, pre, soft, masks, block
    )
    arriving = carry(edge, True, 9)
    gate_low, grad_values, over_edge, chan_grad = rec_back_second(
        beyond, local_grad, arriving, hidden_state, entering, pre, conv_low, rec_chan, soft,
        gates_flat, masks, ext,
    )
    from_next = from_behind(over_edge[:3], "seq", -1)
    grad_values = jnp.concatenate([grad_values[:-3], grad_values[-3:] + from_next]).astype(BF16)
    part = (dot(grad_values, rec_in[:, 0], (1, 1)) + dot(grad_branch, rec_in[:, 1], (1, 1))).astype(
        BF16
    )
    _, gain_one, grad_inputs = join_backward(
        "keep", part, own_rows(stream), gain[0][0], grad_res_one, 8
    )

    two_halves = half_columns(normed_two)
    grad_q = half_grad(two_halves, query_low).astype(F32)
    grad_kv_out = half_grad(two_halves, kv_low).astype(F32)
    grad_attn_out = half_grad(half_columns(low_two), attended).astype(F32).T

    one_halves = half_columns(normed_one)
    grad_in = jnp.stack(
        [half_grad(one_halves, grad_values), half_grad(one_halves, grad_branch)], axis=1
    ).astype(F32)
    grad_rec_out = half_grad(half_columns(mix_low), mixed).astype(F32).T
    gate_parts = jnp.einsum(
        "tnb,ktnc->bnkc",
        conv_low.reshape(count, blocks, block),
        gate_low.reshape(2, count, blocks, block),
        preferred_element_type=F32,
    ).reshape(block, blocks * 2 * block)
    gate_sum = lax.psum_scatter(
        gate_parts.astype(BF16), ("section", "seq"), scatter_dimension=0, tiled=True
    )
    grad_gates = jnp.swapaxes(gate_sum.astype(F32).reshape(-1, blocks, 2, block), 0, 1)
    chan_total = lax.psum(chan_grad, ("section", "seq"))
    grad_chan = jnp.where(first, chan_total[:4], chan_total[4:])

    own_part_in = jnp.where(first, grads_a[0], grads_b[0])
    other_part_in = swapped(jnp.where(first, grads_b[0], grads_a[0]))
    grad_mlp_in = jnp.stack(
        [
            jnp.where(first, own_part_in, other_part_in),
            jnp.where(first, other_part_in, own_part_in),
        ],
        axis=1,
    ).astype(F32)
    own_part_out = jnp.where(first, grads_a[1], grads_b[1])
    other_part_out = swapped(jnp.where(first, grads_b[1], grads_a[1]))
    grad_mlp_out = jnp.concatenate(
        [
            jnp.where(first, own_part_out, other_part_out).T,
            jnp.where(first, other_part_out, own_part_out).T,
        ],
        axis=0,
    ).astype(F32)

    gain_rows = jnp.concatenate([gain_one, gain_a, gain_two, gain_b], axis=0)
    gain_total = lax.psum(gain_rows, ("section", "seq", "head")).reshape(2, 2, width)
    share = width // blocks_seq
    grad_norms = lax.dynamic_slice_in_dim(pick(gain_total, core), place * share, share, axis=1)

    return (
        final[None],
        grad_inputs.astype(F32)[None],
        grad_norms[None],
        grad_in,
        grad_gates,
        grad_chan,
        grad_rec_out,
        grad_q,
        grad_kv_out,
        grad_attn_out,
        grad_mlp_in[None],
        grad_mlp_out[None],
    )


def solution(mesh):
    in_specs = (
        P(None, "seq", None),
        P(None, "seq"),
        P("section", None, None),
        P(None, None, "head"),
        P("head", None, None, None),
        P(None, "head"),
        P("head", None),
        P(None, "head"),
        P(),
        P("head", None),
        P("section", None, None, "head"),
        P("section", "head", None),
        P(None, "seq", None),
    )
    out_specs = (
        P("section", "seq", None),
        P("section", "seq", None),
        P("section", None, "seq"),
        P(("section", "seq"), None, "head"),
        P("head", ("section", "seq"), None, None),
        P("section", "head"),
        P("head", ("section", "seq")),
        P(("section", "seq"), "head"),
        P(("section", "seq"), None),
        P("head", ("section", "seq")),
        P("section", "seq", None, "head"),
        P("section", "head", "seq"),
    )
    return jax.shard_map(
        on_device, mesh=mesh, in_specs=in_specs, out_specs=out_specs, check_vma=False
    )
```

time: 2850 us -> 756 us (0.27)
  waiting for transfers between devices: 1670 us -> 203 us
  local copies, waits for them, and re-layouts: 550 us -> 52.2 us
  other arithmetic: 287 us -> 41.3 us
  Pallas kernels: 0 us -> 224 us
  matrix products: 167 us -> 103 us
  starting transfers between devices: 59.4 us -> 22.3 us
    reduce_scatter x14 -> x9, waiting for transfers between devices: 805 us -> 183 us  [the longest x8 183 us: seq_scatter(): return lax.psum_scatter(grad, 'seq', scatter_dimension=0, tiled=True)]
    psum x7 -> x1, waiting for transfers between devices: 495 us -> 0.02 us  [on_device(): kv_low = lax.psum(kv_part.astype(F32), 'head').astype(BF16)]
    unnamed x39 -> x14, waiting for transfers between devices: 340 us -> 0.92 us
    pallas_call x0 -> x13, Pallas kernels: none -> 224 us  [the longest x4 99.6 us: join_backward(): pl.pallas_call(functools.partial(backward_body, n, kind), name=f'join_bac...]
    slice x118 -> x7, local copies, waits for them, and re-layouts: 223 us -> 2.71 us  [the longest x2 1.22 us: on_device(): gain = [[gains[l][k][None] for k in range(2)] for l in range(2)]]
    pad x56 -> x0, local copies, waits for them, and re-layouts: 126 us -> none  [the longest x28 63 us: rec_backward(): lax.associative_scan(affine, (following, grad_hidden), reverse=True, axis=1)]
    add x55 -> x2, other arithmetic: 80.9 us -> 0.01 us  [the longest x1 0.01 us: attend(): return (attended, row_max[:, :, 0] + jnp.log(row_total[:, :, 0]))]
    dot_general x44 -> x43, matrix products: 155 us -> 97.7 us  [the longest x38 84.3 us: dot(): lax.dot_general(a, b, ((dims[:1], dims[1:]), ((), ())), preferred_element...]
  transfers between devices with their start and end apart: 56 -> 42, of which waited for: 34 -> 17; matrix products, arithmetic and copies ran while one was open for 10% -> 22% of each run, Pallas kernels for 0% -> 27%
where the time goes in v1:
time: 756 us; the launch traced here: 746 us
  Pallas kernels  224 us (30%)
  waiting for transfers between devices  203 us (27%)
  matrix products  103 us (14%)
  blocking collectives  83 us (11%)
  local copies, waits for them, and re-layouts  52.2 us (7%)
  other arithmetic  41.3 us (5%)
  starting transfers between devices  22.3 us (3%)
  between operations  17.3 us (2%)
    reduce_scatter x8, waiting for transfers between devices, seq_scatter(): return lax.psum_scatter(grad, 'seq', scatter_dimension=0, tiled=True)  183 us
    pallas_call x4, Pallas kernels, join_backward(): pl.pallas_call(functools.partial(backward_body, n, kind), name=f'join_bac...  99.6 us
    pallas_call x4, Pallas kernels, join_forward(): pl.pallas_call(functools.partial(forward_body, n, kind), name=f'join_forw...  93.9 us
    dot_general x38, matrix products, dot(): lax.dot_general(a, b, ((dims[:1], dims[1:]), ((), ())), preferred_element...  84.3 us
    psum x1, blocking collectives, on_device(): lax.psum(gain_rows, ('section', 'seq', 'head')).reshape(2, 2, width)  40.8 us
    unnamed x129, local copies, waits for them, and re-layouts  35.9 us
    psum x1, blocking collectives, on_device(): chan_total = lax.psum(chan_grad, ('section', 'seq'))  30.1 us
    ppermute x8, starting transfers between devices, from_behind(): return lax.ppermute(array, axis, pairs)  16.3 us
  transfers between devices with their start and end apart: 42, of which 17 were waited for; matrix products, arithmetic and copies ran while one was open for 22% of the time, Pallas kernels for 27%

profile of v1, /device:TPU:0, one launch (start us, length us, event | category | flops | bytes accessed | tf_op | source)
XLA Modules:
  0.0 746.3 jit_solution(11076281503433235518)
XLA Ops:
  8.1 7.0 copy.121
  16.1 12.2 %all-gather = s32[4,1,256]{2,1,0:T(1,128)S(1)} all-gather(s32[1,1,256]{2,1,0:T(1,128)S(1)} %fusion.206), channel_id=1, replica_groups=mesh['section'=2,'seq'=4,'head'=4] {'seq'}, dimensions={0}, use_global_device_ids=true | all-gather | bytes 5120 | tf_op jit(solution)/shard_map/all_gather | solution.py:557
  36.7 3.2 fusion.135
  43.9 4.9 rec_forward_local.1
  48.8 7.6 %carry_0.1.entering = f32[8,512]{1,0:T(8,128)} custom-call(f32[8,512]{1,0:T(8,128)} %get-tuple-element.45.edge), custom_call_target="tpu_custom_call" | custom-call | tf_op jit(solution)/shard_map/carry_0/pallas_call | solution.py:193
  58.9 2.4 fusion.91
  61.3 2.4 convolution_convert_fusion.1.part
  63.7 22.3 %join_forward_1.1 = (f32[64,1536]{1,0:T(8,128)}, bf16[256,1536]{1,0:T(8,128)(2,1)}) custom-call(bf16[256,1536]{1,0:T(8,128)(2,1)} %convolution_convert_fusion.1.part, f32[64,1536]{1,0:T(8,128)} %dynamic-slice_bitcast_fusion.1.base, f32[1,1536]{1,0:T(1,128)} %get-tuple-element.131.gain), custom_call_target="tpu_custom_call" | custom-call | tf_op jit(solution)/shard_map/join_forward_1/pallas_call | solution.py:133
  86.1 9.3 %broadcast_select_fusion.1 = (bf16[1536,2,1152]{2,0,1:T(8,128)(2,1)S(1)}, bf16[1536,2,1152]{2,0,1:T(8,128)(2,1)}) fusion(bf16[1536,2,1152]{2,0,1:T(8,128)(2,1)} %collective-permute-done.2, pred[]{:T(512)S(6)} %eq.32, bf16[1,1536,2,1152]{3,2,1,0:T(2,128)(2,1)} %param.23), kind=kLoop, calls=%fused_computation.6 | loop fusion | flops 7077888 | bytes 28311552 | tf_op jit(solution)/shard_map/jit(_where)/select_n | solution.py:550
  99.7 4.3 convolution_convert_fusion.3.part
  104.0 22.4 %join_forward_2.1 = (f32[64,1536]{1,0:T(8,128)}, bf16[256,1536]{1,0:T(8,128)(2,1)}) custom-call(bf16[256,1536]{1,0:T(8,128)(2,1)} %convolution_convert_fusion.3.part, f32[64,1536]{1,0:T(8,128)} %get-tuple-element.47.base, f32[1,1536]{1,0:T(1,128)} %get-tuple-element.133.gain), custom_call_target="tpu_custom_call" | custom-call | tf_op jit(solution)/shard_map/join_forward_2/pallas_call | solution.py:133
  128.2 3.3 collective-permute-start.6
  131.5 3.9 collective-permute-start.5
  135.4 2.4 collective-permute-start.4
  137.8 2.5 convolution_convert_fusion.6
  148.5 25.5 %join_forward_3.1 = (f32[64,1536]{1,0:T(8,128)}, bf16[256,1536]{1,0:T(8,128)(2,1)}) custom-call(bf16[256,1536]{1,0:T(8,128)(2,1)} %convolution_convert_fusion.part, f32[64,1536]{1,0:T(8,128)} %get-tuple-element.49.base, f32[1,1536]{1,0:T(1,128)} %get-tuple-element.132.gain), custom_call_target="tpu_custom_call" | custom-call | tf_op jit(solution)/shard_map/join_forward_3/pallas_call | solution.py:133
  174.0 5.4 fusion.73
  179.4 6.8 broadcast_select_fusion.10
  189.5 21.1 %join_backward_5.1 = (f32[64,1536]{1,0:T(8,128)}, f32[1,1536]{1,0:T(1,128)}, bf16[256,1536]{1,0:T(8,128)(2,1)}) custom-call(bf16[256,1536]{1,0:T(8,128)(2,1)} %fusion.15.part, f32[64,1536]{1,0:T(8,128)} %get-tuple-element.51.base, f32[1,1536]{1,0:T(1,128)} %get-tuple-element.132.gain, f32[64,1536]{1,0:T(8,128)} %dynamic-slice_convert_fusion.1.up), custom_call_target="tpu_custom_call" | custom-call | tf_op jit(solution)/shard_map/join_backward_5/pallas_call | solution.py:151
  213.0 2.8 fusion.6
  225.2 4.2 collective-permute-done.9
  229.5 3.9 collective-permute-done.8
  233.5 3.0 fusion.12.part
  237.2 26.6 %join_backward_6.1 = (f32[64,1536]{1,0:T(8,128)}, f32[1,1536]{1,0:T(1,128)}, bf16[256,1536]{1,0:T(8,128)(2,1)}) custom-call(bf16[256,1536]{1,0:T(8,128)(2,1)} %fusion.12.part, f32[64,1536]{1,0:T(8,128)} %get-tuple-element.49.base, f32[1,1536]{1,0:T(1,128)} %get-tuple-element.133.gain, f32[64,1536]{1,0:T(8,128)} %get-tuple-element.54.up), custom_call_target="tpu_custom_call" | custom-call | tf_op jit(solution)/shard_map/join_backward_6/pallas_call | solution.py:151
  263.8 5.7 broadcast_select_fusion.11
  269.5 3.6 fusion.2
  273.2 4.1 fusion.14.part
  277.3 26.2 %join_backward_7.1 = (f32[64,1536]{1,0:T(8,128)}, f32[1,1536]{1,0:T(1,128)}, bf16[256,1536]{1,0:T(8,128)(2,1)}) custom-call(bf16[256,1536]{1,0:T(8,128)(2,1)} %fusion.14.part, f32[64,1536]{1,0:T(8,128)} %get-tuple-element.47.base, f32[1,1536]{1,0:T(1,128)} %get-tuple-element.131.gain, f32[64,1536]{1,0:T(8,128)} %get-tuple-element.56.up), custom_call_target="tpu_custom_call" | custom-call | tf_op jit(solution)/shard_map/join_backward_7/pallas_call | solution.py:151
  303.5 3.0 fusion.138.gm
  306.6 4.5 rec_back_first.1
  311.1 8.5 %carry_9.1.arriving = f32[8,512]{1,0:T(8,128)} custom-call(f32[8,512]{1,0:T(8,128)} %get-tuple-element.61.edge), custom_call_target="tpu_custom_call" | custom-call | tf_op jit(solution)/shard_map/carry_9/pallas_call | solution.py:193
  319.6 5.3 rec_back_second.1
  362.3 3.1 fusion
  367.0 2.6 collective-permute-done.24
  370.9 3.1 fusion.1
  376.1 4.0 copy.65
  387.8 5.2 convolution_convert_fusion.2.part
  393.0 23.7 %join_forward_4.1 = (f32[64,1536]{1,0:T(8,128)}, bf16[256,1536]{1,0:T(8,128)(2,1)}) custom-call(bf16[256,1536]{1,0:T(8,128)(2,1)} %convolution_convert_fusion.2.part, f32[64,1536]{1,0:T(8,128)} %get-tuple-element.51.base, f32[1,1536]{1,0:T(1,128)} %get-tuple-element.132.gain), custom_call_target="tpu_custom_call" | custom-call | tf_op jit(solution)/shard_map/join_forward_4/pallas_call | solution.py:133
  416.7 30.1 %psum.22 = f32[8,512]{1,0:T(8,128)S(1)} all-reduce(f32[8,512]{1,0:T(8,128)S(1)} %copy-done.48), channel_id=1, replica_groups=mesh['section'=2,'seq'=4,'head'=4] {'section','seq'}, use_global_device_ids=true, to_apply=%region_8.9 | all-reduce | flops 4096 | bytes 32768 | tf_op jit(solution)/shard_map/psum | solution.py:697
  457.0 25.7 %join_backward_8.1 = (f32[64,1536]{1,0:T(8,128)}, f32[1,1536]{1,0:T(1,128)}, bf16[256,1536]{1,0:T(8,128)(2,1)}) custom-call(bf16[256,1536]{1,0:T(8,128)(2,1)} %fusion.13.part, f32[64,1536]{1,0:T(8,128)} %dynamic-slice_bitcast_fusion.1.base, f32[1,1536]{1,0:T(1,128)} %get-tuple-element.129.gain, f32[64,1536]{1,0:T(8,128)} %get-tuple-element.66.up), custom_call_target="tpu_custom_call" | custom-call | tf_op jit(solution)/shard_map/join_backward_8/pallas_call | solution.py:151
  483.6 40.8 %psum.21 = f32[2,2,1536]{2,1,0:T(2,128)S(1)} all-reduce(f32[2,2,1536]{2,1,0:T(2,128)S(1)} %reshape.231), channel_id=1, replica_groups=mesh['section'=2,'seq'=4,'head'=4] {'section','seq','head'}, use_global_device_ids=true, to_apply=%region_4.5 | all-reduce | flops 6144 | bytes 49152 | tf_op jit(solution)/shard_map/psum | solution.py:720
  527.4 2.5 bitcast_convert_fusion
  539.6 41.9 %reduce-scatter.30.cloned.1.call-done = bf16[384,1152]{1,0:T(8,128)(2,1)} async-done(((bf16[1536,1152]{1,0:T(8,128)(2,1)}), bf16[384,1152]{1,0:T(8,128)(2,1)}) %reduce-scatter.30.cloned.1.call-update) | async-done | bytes 884752 | tf_op jit(solution)/shard_map/reduce_scatter | solution.py:497
  581.5 69.4 %reduce-scatter.32.cloned.1.call-done = bf16[384,1152]{1,0:T(8,128)(2,1)} async-done(((bf16[1536,1152]{1,0:T(8,128)(2,1)}), bf16[384,1152]{1,0:T(8,128)(2,1)}) %reduce-scatter.32.cloned.1.call-update) | async-done | bytes 884752 | tf_op jit(solution)/shard_map/reduce_scatter | solution.py:497
  653.1 23.9 %reduce-scatter.18.cloned.1.call-done = bf16[192,512]{1,0:T(8,128)(2,1)} async-done(((bf16[768,512]{1,0:T(8,128)(2,1)}), bf16[192,512]{1,0:T(8,128)(2,1)}) %reduce-scatter.18.cloned.1.call-update) | async-done | bytes 196624 | tf_op jit(solution)/shard_map/reduce_scatter | solution.py:497
  677.0 25.6 %reduce-scatter.16.cloned.1.call-done = bf16[192,512]{1,0:T(8,128)(2,1)} async-done(((bf16[768,512]{1,0:T(8,128)(2,1)}), bf16[192,512]{1,0:T(8,128)(2,1)}) %reduce-scatter.16.cloned.1.call-update) | async-done | bytes 196624 | tf_op jit(solution)/shard_map/reduce_scatter | solution.py:497
  705.2 22.3 %reduce-scatter.22.cloned.1.call-done = bf16[192,512]{1,0:T(8,128)(2,1)} async-done(((bf16[768,512]{1,0:T(8,128)(2,1)}), bf16[192,512]{1,0:T(8,128)(2,1)}) %reduce-scatter.22.cloned.1.call-update) | async-done | bytes 196624 | tf_op jit(solution)/shard_map/reduce_scatter | solution.py:497
  732.9 4.5 copy.87
  (314 shorter events, 130.2 us)
Async XLA Ops:
  8.0 24.1 %copy-start = (bf16[2,256,1536]{2,1,0:T(8,128)(2,1)S(1)}, bf16[2,256,1536]{2,1,0:T(8,128)(2,1)}, u32[]{:S(2)}) copy-start(bf16[2,256,1536]{2,1,0:T(8,128)(2,1)} %param.25) | copy-start | bytes 4718596
  8.0 20.2 %copy-start.16 = (bf16[2,256,1536]{2,1,0:T(8,128)(2,1)S(1)}, bf16[2,256,1536]{2,1,0:T(8,128)(2,1)}, u32[]{:S(2)}) copy-start(bf16[2,256,1536]{2,1,0:T(8,128)(2,1)} %param.13) | copy-start | bytes 4718596
  15.0 71.0 %collective-permute-start.2 = (bf16[1536,2,1152]{2,0,1:T(8,128)(2,1)}, bf16[1536,2,1152]{2,0,1:T(8,128)(2,1)}, u32[]{:S(2)}, u32[]{:S(2)}) collective-permute-start(bf16[1536,2,1152]{2,0,1:T(8,128)(2,1)} %bitcast.280), channel_id=1, source_target_pairs={{0,16},{16,0},{1,17},{17,1},{2,18},{18,2},{3,19},{19,3},{4,20},{20... | collective-permute-start | bytes 21233672 | tf_op jit(solution)/shard_map/ppermute | solution.py:434
  15.5 19.1 %collective-permute-start = (f32[2,1536]{1,0:T(2,128)S(1)}, f32[2,1536]{1,0:T(2,128)S(1)}, u32[]{:S(2)}, u32[]{:S(2)}) collective-permute-start(f32[2,1536]{1,0:T(2,128)S(1)} %bitcast.303), channel_id=1, source_target_pairs={{0,16},{16,0},{1,17},{17,1},{2,18},{18,2},{3,19},{19,3},{4,20},{20... | collective-permute-start | bytes 36872 | tf_op jit(solution)/shard_map/ppermute | solution.py:434
  15.5 84.1 %collective-permute-start.3 = (bf16[1152,1536]{1,0:T(8,128)(2,1)}, bf16[1152,1536]{1,0:T(8,128)(2,1)}, u32[]{:S(2)}, u32[]{:S(2)}) collective-permute-start(bf16[1152,1536]{1,0:T(8,128)(2,1)} %bitcast.21), channel_id=1, source_target_pairs={{0,16},{16,0},{1,17},{17,1},{2,18},{18,2},{3,19},{19,3},{4,20},{20... | collective-permute-start | bytes 10616840 | tf_op jit(solution)/shard_map/ppermute | solution.py:434
  39.8 2.8 collective-permute-start.1
  128.2 14.0 %collective-permute-start.6 = (bf16[256,256]{1,0:T(8,128)(2,1)S(1)}, bf16[256,256]{1,0:T(8,128)(2,1)}, u32[]{:S(2)}, u32[]{:S(2)}) collective-permute-start(bf16[256,256]{1,0:T(8,128)(2,1)S(1)} %convolution_convert_fusion.7), channel_id=1, source_target_pairs={{0,4},{4,8},{8,12},{1,5},{5,9},{9,13},{2,6},{6,10},{10,14},{3,7},{... | collective-permute-start | bytes 393224 | tf_op jit(solution)/shard_map/ppermute | solution.py:430
  131.5 10.7 %collective-permute-start.5 = (bf16[256,256]{1,0:T(8,128)(2,1)S(1)}, bf16[256,256]{1,0:T(8,128)(2,1)}, u32[]{:S(2)}, u32[]{:S(2)}) collective-permute-start(bf16[256,256]{1,0:T(8,128)(2,1)S(1)} %convolution_convert_fusion.7), channel_id=1, source_target_pairs={{0,8},{4,12},{1,9},{5,13},{2,10},{6,14},{3,11},{7,15},{16,24},{20,... | collective-permute-start | bytes 393224 | tf_op jit(solution)/shard_map/ppermute | solution.py:430
  135.4 6.8 collective-permute-start.4
  142.2 188.1 %collective-permute-start.16 = (bf16[256,768]{1,0:T(8,128)(2,1)}, bf16[256,768]{1,0:T(8,128)(2,1)}, u32[]{:S(2)}, u32[]{:S(2)}) collective-permute-start(bf16[256,768]{1,0:T(8,128)(2,1)} %constant_dynamic-slice_fusion.3), channel_id=1, source_target_pairs={{0,16},{16,0},{1,17},{17,1},{2,18},{18,2},{3,19},{19,3},{4,20},{20... | collective-permute-start | bytes 1179656 | tf_op jit(solution)/shard_map/ppermute | solution.py:434
  219.3 10.2 %collective-permute-start.9 = (bf16[256,256]{0,1:T(8,128)(2,1)S(1)}, bf16[256,256]{0,1:T(8,128)(2,1)S(1)}, u32[]{:S(2)}, u32[]{:S(2)}) collective-permute-start(bf16[256,256]{0,1:T(8,128)(2,1)S(1)} %get-tuple-element.125), channel_id=1, source_target_pairs={{12,0},{13,1},{14,2},{15,3},{28,16},{29,17},{30,18},{31,19}} | collective-permute-start | bytes 393224 | tf_op jit(solution)/shard_map/ppermute | solution.py:430
  220.7 12.7 %collective-permute-start.8 = (bf16[256,256]{0,1:T(8,128)(2,1)S(1)}, bf16[256,256]{0,1:T(8,128)(2,1)S(1)}, u32[]{:S(2)}, u32[]{:S(2)}) collective-permute-start(bf16[256,256]{0,1:T(8,128)(2,1)S(1)} %get-tuple-element.126), channel_id=1, source_target_pairs={{8,0},{12,4},{9,1},{13,5},{10,2},{14,6},{11,3},{15,7},{24,16},{28,... | collective-permute-start | bytes 393224 | tf_op jit(solution)/shard_map/ppermute | solution.py:430
  222.2 11.2 %collective-permute-start.7 = (bf16[256,256]{0,1:T(8,128)(2,1)S(1)}, bf16[256,256]{0,1:T(8,128)(2,1)S(1)}, u32[]{:S(2)}, u32[]{:S(2)}) collective-permute-start(bf16[256,256]{0,1:T(8,128)(2,1)S(1)} %get-tuple-element.124), channel_id=1, source_target_pairs={{4,0},{8,4},{12,8},{5,1},{9,5},{13,9},{6,2},{10,6},{14,10},{7,3},{... | collective-permute-start | bytes 393224 | tf_op jit(solution)/shard_map/ppermute | solution.py:430
  236.5 92.5 %all-reduce.2.cloned.1.call-start = ((), (), s32[]{:S(2)}) async-start(), calls=%async_computation.16 | async-start | bytes 262144 | tf_op jit(solution)/shard_map/psum | solution.py:649
  237.2 292.6 %reduce-scatter.20.cloned.1.call-start = ((), (), s32[]{:S(2)}) async-start(), calls=%async_computation.13 | async-start | bytes 294912 | tf_op jit(solution)/shard_map/reduce_scatter | solution.py:693
  328.9 202.4 %reduce-scatter.26.cloned.1.call-start = ((), (), s32[]{:S(2)}) async-start(), calls=%async_computation.17 | async-start | bytes 491520 | tf_op jit(solution)/shard_map/reduce_scatter | solution.py:497
  329.0 1.6 collective-permute-start.18
  332.7 200.2 %reduce-scatter.24.cloned.1.call-start = ((), (), s32[]{:S(2)}) async-start(), calls=%async_computation.15 | async-start | bytes 737280 | tf_op jit(solution)/shard_map/reduce_scatter | solution.py:497
  332.7 1.5 collective-permute-start.17
  336.5 198.0 %reduce-scatter.28.cloned.1.call-start = ((), (), s32[]{:S(2)}) async-start(), calls=%async_computation.18 | async-start | bytes 737280 | tf_op jit(solution)/shard_map/reduce_scatter | solution.py:497
  337.3 2.2 collective-permute-start.19
  337.5 2.0 collective-permute-start.20
  341.8 194.3 %reduce-scatter.36.cloned.1.call-start = ((), (), s32[]{:S(2)}) async-start(), calls=%async_computation.22 | async-start | bytes 2457600
  344.3 1.7 collective-permute-start.28
  349.1 188.4 %reduce-scatter.34.cloned.1.call-start = ((), (), s32[]{:S(2)}) async-start(), calls=%async_computation.21 | async-start | bytes 2457600
  350.2 2.8 collective-permute-start.26
  350.6 2.4 collective-permute-start.27
  356.8 224.7 %reduce-scatter.30.cloned.1.call-start = ((), (), s32[]{:S(2)}) async-start(), calls=%async_computation.19 | async-start | bytes 4423680 | tf_op jit(solution)/shard_map/reduce_scatter | solution.py:497
  357.9 2.3 collective-permute-start.21
  358.1 2.9 collective-permute-start.22
  365.4 285.5 %reduce-scatter.32.cloned.1.call-start = ((), (), s32[]{:S(2)}) async-start(), calls=%async_computation.20 | async-start | bytes 4423680 | tf_op jit(solution)/shard_map/reduce_scatter | solution.py:497
  366.5 3.1 collective-permute-start.23
  366.7 2.9 collective-permute-start.24
  374.0 303.0 %reduce-scatter.18.cloned.1.call-start = ((), (), s32[]{:S(2)}) async-start(), calls=%async_computation.12 | async-start | bytes 983040 | tf_op jit(solution)/shard_map/reduce_scatter | solution.py:497
  375.9 8.1 %collective-permute-start.11 = (bf16[256,768]{1,0:T(8,128)(2,1)}, bf16[256,768]{1,0:T(8,128)(2,1)S(1)}, u32[]{:S(2)}, u32[]{:S(2)}) collective-permute-start(bf16[256,768]{1,0:T(8,128)(2,1)} %constant_dynamic-slice_fusion.5), channel_id=1, source_target_pairs={{0,16},{16,0},{1,17},{17,1},{2,18},{18,2},{3,19},{19,3},{4,20},{20... | collective-permute-start | bytes 1179656 | tf_op jit(solution)/shard_map/ppermute | solution.py:434
  380.1 144.9 %collective-permute-start.15 = (bf16[256,512]{1,0:T(8,128)(2,1)}, bf16[256,512]{1,0:T(8,128)(2,1)}, u32[]{:S(2)}, u32[]{:S(2)}) collective-permute-start(bf16[256,512]{1,0:T(8,128)(2,1)} %get-tuple-element.116), channel_id=1, source_target_pairs={{0,16},{16,0},{1,17},{17,1},{2,18},{18,2},{3,19},{19,3},{4,20},{20... | collective-permute-start | bytes 786440 | tf_op jit(solution)/shard_map/ppermute | solution.py:434
  380.4 5.5 collective-permute-start.10
  382.5 1.7 collective-permute-start.13
  385.5 317.1 %reduce-scatter.16.cloned.1.call-start = ((), (), s32[]{:S(2)}) async-start(), calls=%async_computation.11 | async-start | bytes 983040 | tf_op jit(solution)/shard_map/reduce_scatter | solution.py:497
  387.7 29.0 %copy-start.48 = (f32[8,512]{1,0:T(8,128)S(1)}, f32[8,512]{1,0:T(8,128)}, u32[]{:S(2)}) copy-start(f32[8,512]{1,0:T(8,128)} %get-tuple-element.73) | copy-start | bytes 49156
  387.7 59.7 %collective-permute-start.12 = (bf16[256,512]{1,0:T(8,128)(2,1)S(1)}, bf16[256,512]{1,0:T(8,128)(2,1)}, u32[]{:S(2)}, u32[]{:S(2)}) collective-permute-start(bf16[256,512]{1,0:T(8,128)(2,1)S(1)} %pad_maximum_fusion.3), channel_id=1, source_target_pairs={{0,16},{16,0},{1,17},{17,1},{2,18},{18,2},{3,19},{19,3},{4,20},{20... | collective-permute-start | bytes 786440 | tf_op jit(solution)/shard_map/ppermute | solution.py:434
  450.1 277.4 %reduce-scatter.22.cloned.1.call-start = ((), (), s32[]{:S(2)}) async-start(), calls=%async_computation.14 | async-start | bytes 983040 | tf_op jit(solution)/shard_map/reduce_scatter | solution.py:497
  451.0 74.0 %collective-permute-start.14 = (bf16[256,768]{1,0:T(8,128)(2,1)}, bf16[256,768]{1,0:T(8,128)(2,1)}, u32[]{:S(2)}, u32[]{:S(2)}) collective-permute-start(bf16[256,768]{1,0:T(8,128)(2,1)} %constant_dynamic-slice_fusion.4), channel_id=1, source_target_pairs={{0,16},{16,0},{1,17},{17,1},{2,18},{18,2},{3,19},{19,3},{4,20},{20... | collective-permute-start | bytes 1179656 | tf_op jit(solution)/shard_map/ppermute | solution.py:434
  457.0 25.8 %copy-start.50 = (f32[1,1536]{1,0:T(1,128)S(1)}, f32[1,1536]{1,0:T(1,128)}, u32[]{:S(2)}) copy-start(f32[1,1536]{1,0:T(1,128)} %get-tuple-element.71) | copy-start | bytes 18436
  457.0 25.8 %copy-start.51 = (f32[1,1536]{1,0:T(1,128)S(1)}, f32[1,1536]{1,0:T(1,128)}, u32[]{:S(2)}) copy-start(f32[1,1536]{1,0:T(1,128)} %get-tuple-element.70) | copy-start | bytes 18436
  457.0 25.8 %copy-start.52 = (f32[1,1536]{1,0:T(1,128)S(1)}, f32[1,1536]{1,0:T(1,128)}, u32[]{:S(2)}) copy-start(f32[1,1536]{1,0:T(1,128)} %get-tuple-element.69) | copy-start | bytes 18436
  539.6 189.7 %collective-permute-start.29 = (bf16[384,576]{0,1:T(8,128)(2,1)}, bf16[384,576]{0,1:T(8,128)(2,1)}, u32[]{:S(2)}, u32[]{:S(2)}) collective-permute-start(bf16[384,576]{0,1:T(8,128)(2,1)} %broadcast_select_fusion.12), channel_id=1, source_target_pairs={{0,16},{16,0},{1,17},{17,1},{2,18},{18,2},{3,19},{19,3},{4,20},{20... | collective-permute-start | bytes 1327112 | tf_op jit(solution)/shard_map/ppermute | solution.py:434
  653.1 78.6 %collective-permute-start.25 = (bf16[384,1152]{1,0:T(8,128)(2,1)}, bf16[384,1152]{1,0:T(8,128)(2,1)S(1)}, u32[]{:S(2)}, u32[]{:S(2)}) collective-permute-start(bf16[384,1152]{1,0:T(8,128)(2,1)} %broadcast_select_fusion.8), channel_id=1, source_target_pairs={{0,16},{16,0},{1,17},{17,1},{2,18},{18,2},{3,19},{19,3},{4,20},{20... | collective-permute-start | bytes 2654216 | tf_op jit(solution)/shard_map/ppermute | solution.py:434
  (53 other events, 179.1 us)
Sparse Core Ops, SparseCore 0:
  240.7 47.7 all-reduce.1
Sparse Core Ops, SparseCore 1:
  329.0 31.0 reduce-scatter.19
  362.2 19.2 reduce-scatter.25
  383.6 20.5 reduce-scatter.23
  406.5 20.5 reduce-scatter.27
  429.4 40.3 reduce-scatter.35
  472.0 41.4 reduce-scatter.33
  515.6 65.8 reduce-scatter.29
  584.3 66.6 reduce-scatter.31
  653.7 23.3 reduce-scatter.17
  679.9 22.7 reduce-scatter.15
  704.8 22.6 reduce-scatter.21

commit v2 on v1

--- a/solution.py
+++ b/solution.py
@@ -44,7 +44,7 @@
     )
 
 
-def scatter_sum(n, me, rows, part, recv, send_sem, recv_sem):
+def scatter_start(n, me, rows, part, recv, send_sem, recv_sem):
     copies = []
     for k in range(1, n):
         peer = lax.rem(me + k, n)
@@ -61,13 +61,20 @@
         )
     for copy in copies:
         copy.start()
+    return copies
+
+
+def scatter_sum(me, rows, part, recv, copies):
     total = part[pl.ds(pl.multiple_of(me * rows, rows), rows)].astype(F32)
     for k, copy in enumerate(copies):
         copy.wait_recv()
         total = total + recv[k].astype(F32)
+    return total
+
+
+def drain(copies):
     for copy in copies:
         copy.wait_send()
-    return total
 
 
 def spread(n, me, rows, value, full, send_sem, recv_sem):
@@ -83,6 +90,10 @@
         )
     for copy in copies:
         copy.start()
+    return copies
+
+
+def finish(copies):
     for copy in copies:
         copy.wait()
 
@@ -91,7 +102,8 @@
     me = lax.axis_index("head")
     rows = base.shape[0]
     meet("head", me, n)
-    fresh = base[...] + scatter_sum(n, me, rows, part, recv, s1, r1)
+    sent = scatter_start(n, me, rows, part, recv, s1, r1)
+    fresh = base[...] + scatter_sum(me, rows, part, recv, sent)
     if kind == "last":
         new[...] = fresh
         out = fresh
@@ -101,14 +113,26 @@
         new[...] = fresh
         out = fresh * lax.rsqrt(jnp.mean(fresh * fresh, axis=-1, keepdims=True) + EPSILON)
         out = out * gain[...]
-    spread(n, me, rows, out.astype(BF16), full, s2, r2)
-
-
-def backward_body(n, kind, part, base, gain, up, res, gain_grad, full, recv, s1, r1, s2, r2):
+    finish(spread(n, me, rows, out.astype(BF16), full, s2, r2))
+    drain(sent)
+
+
+def backward_body(n, kind, part, base, gain, up, *refs):
+    extra = None
+    if kind == "round":
+        extra, res, gain_grad, full, extra_full, recv, s1, r1, s2, r2, extra_recv, s3, r3, s4, r4 = refs
+    else:
+        res, gain_grad, full, recv, s1, r1, s2, r2 = refs
     me = lax.axis_index("head")
     rows = base.shape[0]
     meet("head", me, n)
-    grad = scatter_sum(n, me, rows, part, recv, s1, r1)
+    if extra is not None:
+        sent_extra = scatter_start(n, me, rows, extra, extra_recv, s3, r3)
+    sent = scatter_start(n, me, rows, part, recv, s1, r1)
+    if extra is not None:
+        joined = scatter_sum(me, rows, extra, extra_recv, sent_extra)
+        done = spread(n, me, rows, joined.astype(BF16), extra_full, s4, r4)
+    grad = scatter_sum(me, rows, part, recv, sent)
     v = base[...]
     scale = lax.rsqrt(jnp.mean(v * v, axis=-1, keepdims=True) + EPSILON)
     gain_grad[...] = jnp.sum(grad * v * scale, axis=0, keepdims=True)
@@ -119,7 +143,11 @@
     if kind == "round":
         out = out.astype(BF16).astype(F32)
     res[...] = out
-    spread(n, me, rows, out.astype(BF16), full, s2, r2)
+    finish(spread(n, me, rows, out.astype(BF16), full, s2, r2))
+    drain(sent)
+    if extra is not None:
+        finish(done)
+        drain(sent_extra)
 
 
 def boundary_scratch(n, rows, width):
@@ -144,23 +172,305 @@
     )(part, base, gain)
 
 
-def join_backward(kind, part, base, gain, up, ident):
+def join_backward(kind, part, base, gain, up, ident, extra=None):
     n = lax.axis_size("head")
     count, width = part.shape
     rows = base.shape[0]
+    outs = [
+        jax.ShapeDtypeStruct((rows, width), F32),
+        jax.ShapeDtypeStruct((1, width), F32),
+        jax.ShapeDtypeStruct((count, width), BF16),
+    ]
+    scratch = boundary_scratch(n, rows, width)
+    operands = [part, base, gain, up]
+    if extra is not None:
+        outs.append(jax.ShapeDtypeStruct(extra.shape, BF16))
+        scratch += boundary_scratch(n, rows, extra.shape[1])
+        operands.append(extra)
     return pl.pallas_call(
         functools.partial(backward_body, n, kind),
         name=f"join_backward_{ident}",
+        out_shape=tuple(outs),
+        in_specs=[vmem()] * len(operands),
+        out_specs=tuple(vmem() for _ in outs),
+        scratch_shapes=scratch,
+        compiler_params=pltpu.CompilerParams(collective_id=ident, has_side_effects=True),
+    )(*operands)
+
+
+def start_body(n, tail, ids, before, every, s0, r0, send_sem, recv_sem):
+    me = lax.axis_index("seq")
+    meet("seq", me, n)
+    copies = [remote(tail, before, s0, r0, "seq", lax.rem(me + 1, n))]
+    every[me] = ids[...]
+    for k in range(1, n):
+        peer = lax.rem(me + k, n)
+        copies.append(
+            remote(ids, every.at[me], send_sem.at[k - 1], recv_sem.at[k - 1], "seq", peer)
+        )
+    for copy in copies:
+        copy.start()
+    finish(copies)
+
+
+def start_exchange(tail, ids, ident):
+    n = lax.axis_size("seq")
+    return pl.pallas_call(
+        functools.partial(start_body, n),
+        name="start_exchange",
         out_shape=(
-            jax.ShapeDtypeStruct((rows, width), F32),
-            jax.ShapeDtypeStruct((1, width), F32),
+            jax.ShapeDtypeStruct(tail.shape, BF16),
+            jax.ShapeDtypeStruct((n,) + ids.shape, jnp.int32),
+        ),
+        in_specs=[vmem(), vmem()],
+        out_specs=(vmem(), vmem()),
+        scratch_shapes=[
+            pltpu.SemaphoreType.DMA,
+            pltpu.SemaphoreType.DMA,
+            pltpu.SemaphoreType.DMA((n - 1,)),
+            pltpu.SemaphoreType.DMA((n - 1,)),
+        ],
+        compiler_params=pltpu.CompilerParams(collective_id=ident, has_side_effects=True),
+    )(tail, ids)
+
+
+def totals_body(heads, blocks, gains, chan, gain_out, chan_out, *scratch):
+    g1, g2, g3, sum_one, sum_two, c2, c3, csum, sems = scratch
+    head, place, core = lax.axis_index("head"), lax.axis_index("seq"), lax.axis_index("section")
+    barrier = pltpu.get_barrier_semaphore()
+    for axis, me, n in (("head", head, heads), ("seq", place, blocks), ("section", core, 2)):
+        for k in range(1, n):
+            pl.semaphore_signal(
+                barrier, inc=1, device_id={axis: lax.rem(me + k, n)}, device_id_type=MESH
+            )
+    pl.semaphore_wait(barrier, heads + blocks - 1)
+    used = 0
+
+    def exchange(src, slots, axis, me, n):
+        nonlocal used
+        copies = []
+        for k in range(1, n):
+            copies.append(
+                remote(
+                    src, slots.at[k - 1], sems.at[0, used], sems.at[1, used], axis, lax.rem(me + k, n)
+                )
+            )
+            used += 1
+        for copy in copies:
+            copy.start()
+        return copies
+
+    def collect(copies, src, slots):
+        total = src[...]
+        for k, copy in enumerate(copies):
+            copy.wait_recv()
+            total = total + slots[k]
+        return total
+
+    by_head = exchange(gains, g1, "head", head, heads)
+    chan_seq = exchange(chan, c2, "seq", place, blocks)
+    sum_one[...] = collect(by_head, gains, g1)
+    gain_seq = exchange(sum_one, g2, "seq", place, blocks)
+    csum[...] = collect(chan_seq, chan, c2)
+    chan_core = exchange(csum, c3, "section", core, 2)
+    sum_two[...] = collect(gain_seq, sum_one, g2)
+    gain_core = exchange(sum_two, g3, "section", core, 2)
+    chan_out[...] = collect(chan_core, csum, c3)
+    gain_out[...] = collect(gain_core, sum_two, g3)
+    for copy in by_head + chan_seq + gain_seq + chan_core + gain_core:
+        copy.wait_send()
+
+
+def totals(gains, chan, ident):
+    heads, blocks = lax.axis_size("head"), lax.axis_size("seq")
+    gs, cs = gains.shape, chan.shape
+    return pl.pallas_call(
+        functools.partial(totals_body, heads, blocks),
+        name="totals",
+        out_shape=(jax.ShapeDtypeStruct(gs, F32), jax.ShapeDtypeStruct(cs, F32)),
+        in_specs=[vmem(), vmem()],
+        out_specs=(vmem(), vmem()),
+        scratch_shapes=[
+            pltpu.VMEM((heads - 1,) + gs, F32),
+            pltpu.VMEM((blocks - 1,) + gs, F32),
+            pltpu.VMEM((1,) + gs, F32),
+            pltpu.VMEM(gs, F32),
+            pltpu.VMEM(gs, F32),
+            pltpu.VMEM((blocks - 1,) + cs, F32),
+            pltpu.VMEM((1,) + cs, F32),
+            pltpu.VMEM(cs, F32),
+            pltpu.SemaphoreType.DMA((2, heads + 2 * blocks)),
+        ],
+        compiler_params=pltpu.CompilerParams(collective_id=ident, has_side_effects=True),
+    )(gains, chan)
+
+
+def either(core, layer, own, other, run):
+    @pl.when(core[0] == layer)
+    def _():
+        run(*own)
+
+    @pl.when(core[0] != layer)
+    def _():
+        run(*other)
+
+
+def weight_specs(layer, width, units, tile):
+    def at_own(i, core):
+        return jnp.where(core[0] == layer, i, 0)
+
+    def at_other(i, core):
+        return jnp.where(core[0] == layer, 0, i)
+
+    return [
+        pl.BlockSpec((2, width, tile), lambda i, core: (0, 0, at_own(i, core))),
+        pl.BlockSpec((2, width, tile), lambda i, core: (0, 0, at_other(i, core))),
+        pl.BlockSpec((tile, width), lambda i, core: (at_own(i, core), 0)),
+        pl.BlockSpec((tile, width), lambda i, core: (at_other(i, core), 0)),
+    ]
+
+
+def mlp_forward_body(layer, steps, core, x, own_in, other_in, own_out, other_out, gate_up, hidden, part, acc):
+    step = pl.program_id(0)
+
+    @pl.when(step == 0)
+    def _():
+        acc[...] = jnp.zeros_like(acc)
+
+    def run(w_in, w_out):
+        gate = jnp.dot(x[...], w_in[0], preferred_element_type=F32)
+        up = jnp.dot(x[...], w_in[1], preferred_element_type=F32)
+        gate_up[0] = gate
+        gate_up[1] = up
+        low = (gelu_parts(gate)[0] * up).astype(BF16)
+        hidden[...] = low
+        acc[...] += jnp.dot(low, w_out[...], preferred_element_type=F32)
+
+    either(core, layer, (own_in, own_out), (other_in, other_out), run)
+
+    @pl.when(step == steps - 1)
+    def _():
+        part[...] = acc[...].astype(BF16)
+
+
+def mlp_forward(layer, core, x, own_in, other_in, own_out, other_out):
+    count, width = x.shape
+    units = own_out.shape[0]
+    tile = units // 3
+    return pl.pallas_call(
+        functools.partial(mlp_forward_body, layer, 3),
+        name=f"mlp_forward_{layer}",
+        grid_spec=pltpu.PrefetchScalarGridSpec(
+            num_scalar_prefetch=1,
+            grid=(3,),
+            in_specs=[pl.BlockSpec((count, width), lambda i, core: (0, 0))]
+            + weight_specs(layer, width, units, tile),
+            out_specs=(
+                pl.BlockSpec((2, count, tile), lambda i, core: (0, 0, i)),
+                pl.BlockSpec((count, tile), lambda i, core: (0, i)),
+                pl.BlockSpec((count, width), lambda i, core: (0, 0)),
+            ),
+            scratch_shapes=[pltpu.VMEM((count, width), F32)],
+        ),
+        out_shape=(
+            jax.ShapeDtypeStruct((2, count, units), F32),
+            jax.ShapeDtypeStruct((count, units), BF16),
             jax.ShapeDtypeStruct((count, width), BF16),
         ),
-        in_specs=[vmem()] * 4,
-        out_specs=(vmem(), vmem(), vmem()),
-        scratch_shapes=boundary_scratch(n, rows, width),
-        compiler_params=pltpu.CompilerParams(collective_id=ident, has_side_effects=True),
-    )(part, base, gain, up)
+    )(core, x, own_in, other_in, own_out, other_out)
+
+
+def mlp_backward_body(layer, steps, core, low, gate_up, own_in, other_in, own_out, other_out, pair, part, acc):
+    step = pl.program_id(0)
+
+    @pl.when(step == 0)
+    def _():
+        acc[...] = jnp.zeros_like(acc)
+
+    over = (((1,), (1,)), ((), ()))
+
+    def run(w_in, w_out):
+        grad_hidden = lax.dot_general(low[...], w_out[...], over, preferred_element_type=F32)
+        act, slope = gelu_parts(gate_up[0])
+        grad_gate = (grad_hidden * gate_up[1] * slope).astype(BF16)
+        grad_up = (grad_hidden * act).astype(BF16)
+        pair[0] = grad_gate
+        pair[1] = grad_up
+        acc[...] += lax.dot_general(grad_gate, w_in[0], over, preferred_element_type=F32)
+        acc[...] += lax.dot_general(grad_up, w_in[1], over, preferred_element_type=F32)
+
+    either(core, layer, (own_in, own_out), (other_in, other_out), run)
+
+    @pl.when(step == steps - 1)
+    def _():
+        part[...] = acc[...].astype(BF16)
+
+
+def mlp_backward(layer, core, low, gate_up, own_in, other_in, own_out, other_out):
+    count, width = low.shape
+    units = own_out.shape[0]
+    tile = units // 3
+    return pl.pallas_call(
+        functools.partial(mlp_backward_body, layer, 3),
+        name=f"mlp_backward_{layer}",
+        grid_spec=pltpu.PrefetchScalarGridSpec(
+            num_scalar_prefetch=1,
+            grid=(3,),
+            in_specs=[
+                pl.BlockSpec((count, width), lambda i, core: (0, 0)),
+                pl.BlockSpec((2, count, tile), lambda i, core: (0, 0, i)),
+            ]
+            + weight_specs(layer, width, units, tile),
+            out_specs=(
+                pl.BlockSpec((2, count, tile), lambda i, core: (0, 0, i)),
+                pl.BlockSpec((count, width), lambda i, core: (0, 0)),
+            ),
+            scratch_shapes=[pltpu.VMEM((count, width), F32)],
+        ),
+        out_shape=(
+            jax.ShapeDtypeStruct((2, count, units), BF16),
+            jax.ShapeDtypeStruct((count, width), BF16),
+        ),
+    )(core, low, gate_up, own_in, other_in, own_out, other_out)
+
+
+def weight_grad_body(sizes, core, *refs):
+    out = refs[-1]
+    over = (((0,), (0,)), ((), ()))
+    start = 0
+    for t, size in enumerate(sizes):
+        left, left_other, right, right_other = refs[4 * t : 4 * t + 4]
+        total = lax.dot_general(left[...], right[...], over, preferred_element_type=F32)
+        total += lax.dot_general(left_other[...], right_other[...], over, preferred_element_type=F32)
+        out[:, start : start + size] = total.astype(BF16)
+        start += size
+
+
+def weight_grad(name, core, terms, half):
+    count, width = terms[0][0].shape
+    tile = 256
+    steps = width // tile // (2 if half else 1)
+    sizes = [term[2].shape[1] for term in terms]
+    in_specs, operands = [], []
+    for left, left_other, right, right_other in terms:
+        if half:
+            rows = pl.BlockSpec((count, tile), lambda i, core: (0, core[0] * steps + i))
+        else:
+            rows = pl.BlockSpec((count, tile), lambda i, core: (0, i))
+        full = pl.BlockSpec(right.shape, lambda i, core: (0, 0))
+        in_specs += [rows, rows, full, full]
+        operands += [left, left_other, right, right_other]
+    return pl.pallas_call(
+        functools.partial(weight_grad_body, sizes),
+        name=f"weight_grad_{name}",
+        grid_spec=pltpu.PrefetchScalarGridSpec(
+            num_scalar_prefetch=1,
+            grid=(steps,),
+            in_specs=in_specs,
+            out_specs=pl.BlockSpec((tile, sum(sizes)), lambda i, core: (i, 0)),
+        ),
+        out_shape=jax.ShapeDtypeStruct((steps * tile, sum(sizes)), BF16),
+    )(core, *operands)
 
 
 def carry_body(n, reverse, edge, out, every, send_sem, recv_sem):
@@ -241,9 +551,9 @@
     count = conv_out.shape[0]
     block = conv_out.shape[1]
     wide = ext[...].astype(F32)
-    total = chan[4:5] + chan[0:1] * wide[8:]
+    total = chan[4:5] + chan[0:1] * wide[16:]
     for k in range(1, 4):
-        total = total + chan[k : k + 1] * pltpu.roll(wide, k, 0)[8:] * masks[:, k : k + 1]
+        total = total + chan[k : k + 1] * pltpu.roll(wide, k, 0)[16:] * masks[:, k : k + 1]
     low = total.astype(BF16)
     conv_out[...] = low
     pre = jnp.dot(low, gates[0], preferred_element_type=F32)
@@ -264,7 +574,7 @@
 
 
 def rec_forward_local(ext, masks, chan, soft, gates):
-    count, chans = ext.shape[0] - 8, ext.shape[1]
+    count, chans = ext.shape[0] - 16, ext.shape[1]
     blocks, block = gates.shape[:2]
     wide = pl.BlockSpec((count, block), lambda i: (0, i))
     row8 = pl.BlockSpec((8, block), lambda i: (0, i))
@@ -280,7 +590,7 @@
             jax.ShapeDtypeStruct((8, chans), F32),
         ),
         in_specs=[
-            pl.BlockSpec((count + 8, block), lambda i: (0, i)),
+            pl.BlockSpec((count + 16, block), lambda i: (0, i)),
             pl.BlockSpec((count, 4), lambda i: (0, 0)),
             row8,
             row8,
@@ -368,12 +678,12 @@
     )
     wide = ext[...].astype(F32)
     total = chan[0:1] * grad_conv
-    chan_grad[0:1] = jnp.sum(grad_conv * wide[8:], axis=0, keepdims=True)
+    chan_grad[0:1] = jnp.sum(grad_conv * wide[16:], axis=0, keepdims=True)
     row8 = lax.broadcasted_iota(jnp.int32, (8, block), 0)
     over_edge = jnp.zeros((8, block), F32)
     for k in range(1, 4):
         masked = grad_conv * masks[:, k : k + 1]
-        chan_grad[k : k + 1] = jnp.sum(masked * pltpu.roll(wide, k, 0)[8:], axis=0, keepdims=True)
+        chan_grad[k : k + 1] = jnp.sum(masked * pltpu.roll(wide, k, 0)[16:], axis=0, keepdims=True)
         back = chan[k : k + 1] * masked
         total = total + shifted(back, -k, row, 0.0)
         first = back[0:8]
@@ -418,7 +728,7 @@
             row8,
             pl.BlockSpec((1, block, 2 * block), lambda i: (i, 0, 0)),
             pl.BlockSpec((count, 4), lambda i: (0, 0)),
-            pl.BlockSpec((count + 8, block), lambda i: (0, i)),
+            pl.BlockSpec((count + 16, block), lambda i: (0, i)),
         ],
         out_specs=(pair, wide, row8, row8),
     )(beyond, local, arriving, hidden, entering, pre, conv, chan, soft, gates, masks, ext)
@@ -476,29 +786,8 @@
     return (grad_query, jnp.concatenate([grad_keys, grad_values], axis=-1))
 
 
-def mlp_forward(normed, w_in, w_out):
-    gate_up = jnp.einsum("td,dkf->tkf", normed, w_in, preferred_element_type=F32)
-    hidden = (jax.nn.gelu(gate_up[:, 0]) * gate_up[:, 1]).astype(BF16)
-    return gate_up, hidden, dot(hidden, w_out, (1, 0), BF16)
-
-
-def mlp_backward(gate_up, w_in, w_out, out_low):
-    grad_hidden = dot(out_low, w_out, (1, 1))
-    act, slope = gelu_parts(gate_up[:, 0])
-    grad_gate = (grad_hidden * gate_up[:, 1] * slope).astype(BF16)
-    grad_up = (grad_hidden * act).astype(BF16)
-    part = (
-        dot(grad_gate, w_in[:, 0], (1, 1)) + dot(grad_up, w_in[:, 1], (1, 1))
-    ).astype(BF16)
-    return grad_gate, grad_up, part
-
-
 def seq_scatter(grad):
     return lax.psum_scatter(grad, "seq", scatter_dimension=0, tiled=True)
-
-
-def pair_grad(left, left_other, right, right_other):
-    return (dot(left, right, (0, 0)) + dot(left_other, right_other, (0, 0))).astype(BF16)
 
 
 def columns(array, start, size):
@@ -530,7 +819,6 @@
     rows = count // heads
     chans = rec_in.shape[2]
     blocks, block = rec_gates.shape[:2]
-    half_width = width // 2
 
     def pick(array, index):
         return lax.dynamic_index_in_dim(array, index, 0, keepdims=False)
@@ -538,33 +826,29 @@
     def own_rows(array):
         return lax.dynamic_slice_in_dim(array, rank * rows, rows, axis=0)
 
-    def mine_and_other(pair_zero, pair_one):
-        return jnp.where(first, pair_zero, pair_one), swapped(jnp.where(first, pair_one, pair_zero))
-
-    other_in, other_out, other_norms = swapped(mlp_in[0]), swapped(mlp_out[0]), swapped(norms[0])
+    core_ref = core[None].astype(jnp.int32)
+    ids = pick(segments, core)
+    stream_low = pick(inputs, core)
+    top_low = pick(cotangent, core)
+    before, every_id = start_exchange(stream_low[-16:], ids[None], 10)
+    every_id = every_id[:, 0]
+
+    own_in = jnp.swapaxes(mlp_in[0], 0, 1)
+    other_in, other_out, other_norms = swapped(own_in), swapped(mlp_out[0]), swapped(norms[0])
     gains = [
         jnp.where(first, norms[0], other_norms),
         jnp.where(first, other_norms, norms[0]),
     ]
     gain = [[gains[l][k][None] for k in range(2)] for l in range(2)]
-    w_in = [jnp.where(first, mlp_in[0], other_in), jnp.where(first, other_in, mlp_in[0])]
-    w_out = [jnp.where(first, mlp_out[0], other_out), jnp.where(first, other_out, mlp_out[0])]
-
-    stream_low = pick(inputs, core)
-    stream = stream_low.astype(F32)
-    top_low = pick(cotangent, core)
-    ids = pick(segments, core)
-    every_id = lax.all_gather(ids, "seq")
+    weights = (own_in, other_in, mlp_out[0], other_out)
 
     def rooted(x):
         return x * lax.rsqrt(jnp.mean(x * x, axis=-1, keepdims=True) + EPSILON) * gain[0][0]
 
-    normed_one = rooted(stream).astype(BF16)
-    branches = jnp.einsum("td,dkr->ktr", normed_one, rec_in, preferred_element_type=F32)
-    values = branches[0].astype(BF16)
-    gate_pre = branches[1]
-    before = from_behind(values[-8:], "seq", 1)
-    ext = jnp.concatenate([before, values], axis=0)
+    ext_normed = rooted(jnp.concatenate([before, stream_low]).astype(F32)).astype(BF16)
+    normed_one = ext_normed[16:]
+    ext = dot(ext_normed, rec_in[:, 0], (1, 0), BF16)
+    gate_pre = dot(normed_one, rec_in[:, 1], (1, 0))
     before_ids = pick(every_id, jnp.maximum(place - 1, 0))[-3:]
     ext_ids = jnp.concatenate([jnp.where(place == 0, -1, before_ids), ids])
     masks = jnp.stack(
@@ -577,9 +861,10 @@
     hidden_state = local + through * entering[0:1]
     mixed = (hidden_state * jax.nn.gelu(gate_pre)).astype(BF16)
     part = dot(mixed, rec_out, (1, 0), BF16)
-    res_one, normed_a = join_forward("keep", part, own_rows(stream), gain[0][1], 1)
-
-    gate_up_a, hidden_a, part = mlp_forward(normed_a, w_in[0], w_out[0])
+    stream_rows = own_rows(stream_low).astype(F32)
+    res_one, normed_a = join_forward("keep", part, stream_rows, gain[0][1], 1)
+
+    gate_up_a, hidden_a, part = mlp_forward(0, core_ref, normed_a, *weights)
     passed, normed_two = join_forward("round", part, res_one, gain[1][0], 2)
 
     head_dim = attn_kv.shape[1] // 2
@@ -603,31 +888,22 @@
     part = dot(attended, attn_out, (1, 0), BF16)
     res_two, normed_b = join_forward("keep", part, passed, gain[1][1], 3)
 
-    gate_up_b, hidden_b, part = mlp_forward(normed_b, w_in[1], w_out[1])
-    _, final = join_forward("last", part, res_two, gain[1][1], 4)
-
-    def mlp_grads(normed, hidden, grad_gate, grad_up, out_low, out_other):
-        side, side_other = mine_and_other(grad_gate, grad_up)
-        units = hidden.shape[1] // 2
+    gate_up_b, hidden_b, part_last = mlp_forward(1, core_ref, normed_b, *weights)
+
+    units = hidden_b.shape[1] // 2
+
+    def mlp_term(pair, normed, hidden, out_low, out_other):
+        side, side_other = pick(pair, core), swapped(pick(pair, 1 - core))
         kept = columns(hidden, core * units, units)
         kept_other = swapped(columns(hidden, (1 - core) * units, units))
-        grad_in = pair_grad(normed, swapped(normed), side, side_other)
-        grad_out = pair_grad(out_low, out_other, kept, kept_other)
-        return seq_scatter(grad_in), seq_scatter(grad_out)
-
-    def half_columns(array):
-        own = columns(array, core * half_width, half_width)
-        return own, swapped(columns(array, (1 - core) * half_width, half_width))
-
-    def half_grad(array_pair, right):
-        return seq_scatter(pair_grad(array_pair[0], array_pair[1], right, swapped(right)))
-
-    grad_gate_b, grad_up_b, part = mlp_backward(gate_up_b, w_in[1], w_out[1], top_low)
-    grads_b = mlp_grads(
-        normed_b, hidden_b, grad_gate_b, grad_up_b, top_low, pick(cotangent, 1 - core)
-    )
+        return [(normed, swapped(normed), side, side_other), (out_low, out_other, kept, kept_other)]
+
+    pair_b, part = mlp_backward(1, core_ref, top_low, gate_up_b, *weights)
+    terms = mlp_term(pair_b, normed_b, hidden_b, top_low, pick(cotangent, 1 - core))
+    part, sum_b = lax.optimization_barrier((part, weight_grad("b", core_ref, terms, False)))
+    sum_b = seq_scatter(sum_b)
     grad_res_two, gain_b, low_two = join_backward(
-        "keep", part, res_two, gain[1][1], own_rows(top_low.astype(F32)), 5
+        "keep", part, res_two, gain[1][1], own_rows(top_low).astype(F32), 5
     )
 
     grad_att = dot(low_two, attn_out, (1, 1), BF16)
@@ -643,15 +919,28 @@
     query_low = grad_query.reshape(count, heads_here * head_dim).astype(BF16)
     kv_part = own_kv.astype(BF16)
     part = (dot(query_low, attn_q, (1, 1)) + dot(kv_part, attn_kv, (1, 1))).astype(BF16)
-    grad_passed, gain_two, low_passed = join_backward(
-        "round", part, passed, gain[1][0], grad_res_two, 6
-    )
-    kv_low = lax.psum(kv_part.astype(F32), "head").astype(BF16)
-
-    grad_gate_a, grad_up_a, part = mlp_backward(gate_up_a, w_in[0], w_out[0], low_passed)
-    grads_a = mlp_grads(
-        normed_a, hidden_a, grad_gate_a, grad_up_a, low_passed, swapped(low_passed)
-    )
+    grad_passed, gain_two, low_passed, kv_low = join_backward(
+        "round", part, passed, gain[1][0], grad_res_two, 6, kv_part
+    )
+
+    pair_a, part = mlp_backward(0, core_ref, low_passed, gate_up_a, *weights)
+    normed_two_other = swapped(normed_two)
+    attn_sum = weight_grad(
+        "attention",
+        core_ref,
+        [
+            (normed_two, normed_two_other, query_low, swapped(query_low)),
+            (normed_two, normed_two_other, kv_low, swapped(kv_low)),
+            (low_two, swapped(low_two), attended, swapped(attended)),
+        ],
+        True,
+    )
+    terms = mlp_term(pair_a, normed_a, hidden_a, low_passed, swapped(low_passed))
+    part, sum_a, attn_sum = lax.optimization_barrier(
+        (part, weight_grad("a", core_ref, terms, False), attn_sum)
+    )
+    attn_sum = seq_scatter(attn_sum)
+    sum_a = seq_scatter(sum_a)
     grad_res_one, gain_a, mix_low = join_backward(
         "keep", part, res_one, gain[0][1], grad_passed, 7
     )
@@ -670,56 +959,73 @@
     part = (dot(grad_values, rec_in[:, 0], (1, 1)) + dot(grad_branch, rec_in[:, 1], (1, 1))).astype(
         BF16
     )
+    normed_one_other = swapped(normed_one)
+    rec_sum = weight_grad(
+        "recurrent",
+        core_ref,
+        [
+            (normed_one, normed_one_other, grad_values, swapped(grad_values)),
+            (normed_one, normed_one_other, grad_branch, swapped(grad_branch)),
+            (mix_low, swapped(mix_low), mixed, swapped(mixed)),
+        ],
+        True,
+    )
+    side = pick(gate_low, core)
+    side_other = swapped(pick(gate_low, 1 - core))
+    conv_other = swapped(conv_low)
+
+    def gate_grad(left, right):
+        return jnp.einsum(
+            "tnb,tnc->bnc",
+            left.reshape(count, blocks, block),
+            right.reshape(count, blocks, block),
+            preferred_element_type=F32,
+        )
+
+    gate_sum = (gate_grad(conv_low, side) + gate_grad(conv_other, side_other)).astype(BF16)
+    share = block // (2 * blocks_seq)
+    gate_sum = jnp.swapaxes(
+        gate_sum.reshape(2, blocks_seq, share, chans), 0, 1
+    ).reshape(block, chans)
+    part, rec_sum, gate_sum = lax.optimization_barrier((part, rec_sum, gate_sum))
+    rec_sum = seq_scatter(rec_sum)
+    gate_sum = seq_scatter(gate_sum).reshape(2, share, chans)
     _, gain_one, grad_inputs = join_backward(
-        "keep", part, own_rows(stream), gain[0][0], grad_res_one, 8
-    )
-
-    two_halves = half_columns(normed_two)
-    grad_q = half_grad(two_halves, query_low).astype(F32)
-    grad_kv_out = half_grad(two_halves, kv_low).astype(F32)
-    grad_attn_out = half_grad(half_columns(low_two), attended).astype(F32).T
-
-    one_halves = half_columns(normed_one)
-    grad_in = jnp.stack(
-        [half_grad(one_halves, grad_values), half_grad(one_halves, grad_branch)], axis=1
-    ).astype(F32)
-    grad_rec_out = half_grad(half_columns(mix_low), mixed).astype(F32).T
-    gate_parts = jnp.einsum(
-        "tnb,ktnc->bnkc",
-        conv_low.reshape(count, blocks, block),
-        gate_low.reshape(2, count, blocks, block),
-        preferred_element_type=F32,
-    ).reshape(block, blocks * 2 * block)
-    gate_sum = lax.psum_scatter(
-        gate_parts.astype(BF16), ("section", "seq"), scatter_dimension=0, tiled=True
-    )
-    grad_gates = jnp.swapaxes(gate_sum.astype(F32).reshape(-1, blocks, 2, block), 0, 1)
-    chan_total = lax.psum(chan_grad, ("section", "seq"))
+        "keep", part, stream_rows, gain[0][0], grad_res_one, 8
+    )
+    part_last, grad_inputs, gain_one = lax.optimization_barrier((part_last, grad_inputs, gain_one))
+    _, final = join_forward("last", part_last, res_two, gain[1][1], 4)
+
+    gain_rows = jnp.concatenate([gain_one, gain_a, gain_two, gain_b], axis=0)
+    gain_total, chan_total = totals(gain_rows, chan_grad, 11)
+    share_norm = width // blocks_seq
+    grad_norms = lax.dynamic_slice_in_dim(
+        pick(gain_total.reshape(2, 2, width), core), place * share_norm, share_norm, axis=1
+    )
     grad_chan = jnp.where(first, chan_total[:4], chan_total[4:])
 
-    own_part_in = jnp.where(first, grads_a[0], grads_b[0])
-    other_part_in = swapped(jnp.where(first, grads_b[0], grads_a[0]))
-    grad_mlp_in = jnp.stack(
-        [
-            jnp.where(first, own_part_in, other_part_in),
-            jnp.where(first, other_part_in, own_part_in),
-        ],
-        axis=1,
-    ).astype(F32)
-    own_part_out = jnp.where(first, grads_a[1], grads_b[1])
-    other_part_out = swapped(jnp.where(first, grads_b[1], grads_a[1]))
-    grad_mlp_out = jnp.concatenate(
-        [
-            jnp.where(first, own_part_out, other_part_out).T,
-            jnp.where(first, other_part_out, own_part_out).T,
-        ],
-        axis=0,
-    ).astype(F32)
-
-    gain_rows = jnp.concatenate([gain_one, gain_a, gain_two, gain_b], axis=0)
-    gain_total = lax.psum(gain_rows, ("section", "seq", "head")).reshape(2, 2, width)
-    share = width // blocks_seq
-    grad_norms = lax.dynamic_slice_in_dim(pick(gain_total, core), place * share, share, axis=1)
+    chans_q = attn_q.shape[1]
+    attn_sum = attn_sum.astype(F32)
+    grad_q = attn_sum[:, :chans_q]
+    grad_kv_out = attn_sum[:, chans_q : chans_q + 2 * head_dim]
+    grad_attn_out = attn_sum[:, chans_q + 2 * head_dim :].T
+    rec_sum = rec_sum.astype(F32)
+    grad_in = rec_sum[:, : 2 * chans].reshape(-1, 2, chans)
+    grad_rec_out = rec_sum[:, 2 * chans :].T
+    own_gate = pick(gate_sum, core)
+    other_gate = swapped(pick(gate_sum, 1 - core))
+    grad_gates = jnp.transpose(
+        jnp.stack([jnp.where(first, own_gate, other_gate), jnp.where(first, other_gate, own_gate)])
+        .astype(F32)
+        .reshape(2, share, blocks, block),
+        (2, 1, 0, 3),
+    )
+    own_part = jnp.where(first, sum_a, sum_b)
+    other_part = swapped(jnp.where(first, sum_b, sum_a))
+    lower = jnp.where(first, own_part, other_part).astype(F32)
+    upper = jnp.where(first, other_part, own_part).astype(F32)
+    grad_mlp_in = jnp.stack([lower[:, : 2 * units], upper[:, : 2 * units]], axis=1)
+    grad_mlp_out = jnp.concatenate([lower[:, 2 * units :].T, upper[:, 2 * units :].T], axis=0)
 
     return (
         final[None],

time: 756 us -> 583 us (0.77)
  waiting for transfers between devices: 203 us -> 70.5 us
  Pallas kernels: 224 us -> 331 us
  blocking collectives: 83 us -> 0 us
  matrix products: 103 us -> 36.5 us
  local copies, waits for them, and re-layouts: 52.2 us -> 74.3 us
  other arithmetic: 41.3 us -> 23.8 us
    reduce_scatter x8 -> x5, waiting for transfers between devices: 183 us -> 50.5 us  [seq_scatter(): return lax.psum_scatter(grad, 'seq', scatter_dimension=0, tiled=True)]
    pallas_call x0 -> x10, Pallas kernels: none -> 92.5 us  [the longest x4 27.5 us: weight_grad(): pl.pallas_call(functools.partial(weight_grad_body, sizes), name=f'weight_...]
    psum x2 -> x0, blocking collectives: 70.8 us -> none  [the longest x1 40.8 us: on_device(): lax.psum(gain_rows, ('section', 'seq', 'head')).reshape(2, 2, width)]
    dot_general x38 -> x12, matrix products: 84.3 us -> 27.7 us  [dot(): lax.dot_general(a, b, ((dims[:1], dims[1:]), ((), ())), preferred_element...]
    all_gather x1 -> x0, blocking collectives: 12.2 us -> none  [on_device(): every_id = lax.all_gather(ids, 'seq')]
    slice x1 -> x6, local copies, waits for them, and re-layouts: 0.01 us -> 11.8 us  [the longest x1 5.93 us: on_device(): ext = dot(ext_normed, rec_in[:, 0], (1, 0), BF16)]
    unnamed x129 -> x97, local copies, waits for them, and re-layouts: 35.9 us -> 25.3 us
    select_n x3 -> x2, other arithmetic: 12.3 us -> 2.22 us  [the longest x1 1.49 us: on_device(): other_part = swapped(jnp.where(first, sum_b, sum_a))]
  transfers between devices with their start and end apart: 42 -> 36, of which waited for: 17 -> 7; matrix products, arithmetic and copies ran while one was open for 22% -> 17% of each run, Pallas kernels for 27% -> 46%
where the time goes in v2:
time: 583 us; the launch traced here: 573 us
  Pallas kernels  331 us (57%)
  local copies, waits for them, and re-layouts  74.3 us (13%)
  waiting for transfers between devices  70.5 us (12%)
  matrix products  36.5 us (6%)
  other arithmetic  23.8 us (4%)
  starting transfers between devices  21.7 us (4%)
  between operations  15.2 us (3%)
    pallas_call x4, Pallas kernels, join_backward(): pl.pallas_call(functools.partial(backward_body, n, kind), name=f'join_bac...  104 us
    pallas_call x4, Pallas kernels, join_forward(): pl.pallas_call(functools.partial(forward_body, n, kind), name=f'join_forw...  93.4 us
    reduce_scatter x5, waiting for transfers between devices, seq_scatter(): return lax.psum_scatter(grad, 'seq', scatter_dimension=0, tiled=True)  50.5 us
    dot_general x12, matrix products, dot(): lax.dot_general(a, b, ((dims[:1], dims[1:]), ((), ())), preferred_element...  27.7 us
    pallas_call x4, Pallas kernels, weight_grad(): pl.pallas_call(functools.partial(weight_grad_body, sizes), name=f'weight_...  27.5 us
    pallas_call x2, Pallas kernels, carry(): pl.pallas_call(functools.partial(carry_body, n, reverse), name=f'carry_{i...  25.9 us
    unnamed x97, local copies, waits for them, and re-layouts  25.3 us
    pallas_call x2, Pallas kernels, mlp_backward(): pl.pallas_call(functools.partial(mlp_backward_body, layer, 3), name=f'mlp...  22 us
  transfers between devices with their start and end apart: 36, of which 7 were waited for; matrix products, arithmetic and copies ran while one was open for 17% of the time, Pallas kernels for 46%

profile of v2, /device:TPU:0, one launch (start us, length us, event | category | flops | bytes accessed | tf_op | source)
XLA Modules:
  0.0 572.7 jit_solution(10967281161368362407)
XLA Ops:
  7.3 6.8 %copy.144 = bf16[1,1536,2,1152]{3,1,2,0:T(8,128)(2,1)} copy(bf16[1,1536,2,1152]{3,2,1,0:T(2,128)(2,1)} %param.23) | data formatting | bytes 14155776 | tf_op args[10]
  17.1 8.8 %start_exchange.1 = (bf16[16,1536]{1,0:T(8,128)(2,1)}, s32[4,1,256]{2,1,0:T(1,128)}) custom-call(bf16[16,1536]{1,0:T(8,128)(2,1)} %dynamic-slice_bitcast_fusion.8.tail, s32[1,256]{1,0:T(1,128)} %constant_dynamic-slice_fusion.10.ids), custom_call_target="tpu_custom_call" | custom-call | tf_op jit(solution)/shard_map/start_exchange/pallas_call | solution.py:218
  30.5 2.2 fusion.25
  38.3 5.9 %fusion.50 = (bf16[1536,1,512]{2,1,0:T(2,128)(2,1)}, bf16[1536,1,512]{2,1,0:T(2,128)(2,1)}) fusion(bf16[1536,2,512]{2,1,0:T(2,128)(2,1)S(1)} %copy-done.3), kind=kLoop, calls=%fused_computation.140 | loop fusion | bytes 6291456 | tf_op jit(solution)/shard_map/slice | solution.py:850
  46.9 3.5 convolution_convert_fusion.2.ext
  51.0 4.9 rec_forward_local.1
  55.9 7.3 %carry_0.1.entering = f32[8,512]{1,0:T(8,128)} custom-call(f32[8,512]{1,0:T(8,128)} %get-tuple-element.73.edge), custom_call_target="tpu_custom_call" | custom-call | tf_op jit(solution)/shard_map/carry_0/pallas_call | solution.py:503
  63.9 3.8 fusion.36
  67.8 2.4 convolution_convert_fusion.1.part
  70.2 21.5 %join_forward_1.1 = (f32[64,1536]{1,0:T(8,128)}, bf16[256,1536]{1,0:T(8,128)(2,1)}) custom-call(bf16[256,1536]{1,0:T(8,128)(2,1)} %convolution_convert_fusion.1.part, f32[64,1536]{1,0:T(8,128)} %bitcast_convert_fusion.2.base, f32[1,1536]{1,0:T(1,128)} %get-tuple-element.189.gain), custom_call_target="tpu_custom_call" | custom-call | tf_op jit(solution)/shard_map/join_forward_1/pallas_call | solution.py:161
  91.7 10.1 %mlp_forward_0.1 = (f32[2,256,1152]{2,1,0:T(8,128)}, bf16[256,1152]{1,0:T(8,128)(2,1)}, bf16[256,1536]{1,0:T(8,128)(2,1)}) custom-call(s32[1]{0:T(128)} %bitcast.core, bf16[256,1536]{1,0:T(8,128)(2,1)} %get-tuple-element.74.x.refs_0_, bf16[2,1536,1152]{2,1,0:T(8,128)(2,1)} %bitcast.169.own_in, bf16[2,1536,1152]{2,1,0:T(8,128)(2,1)} %collective-permute-done.1.other_in, ...), custom_call_target="tpu_custom_call" | custom-call | tf_op jit(solution)/shard_map/mlp_forward_0/pallas_call | solution.py:360
  101.8 24.2 %join_forward_2.1 = (f32[64,1536]{1,0:T(8,128)}, bf16[256,1536]{1,0:T(8,128)(2,1)}) custom-call(bf16[256,1536]{1,0:T(8,128)(2,1)} %get-tuple-element.75.part, f32[64,1536]{1,0:T(8,128)} %get-tuple-element.76.base, f32[1,1536]{1,0:T(1,128)} %get-tuple-element.203.gain), custom_call_target="tpu_custom_call" | custom-call | tf_op jit(solution)/shard_map/join_forward_2/pallas_call | solution.py:161
  127.5 3.1 collective-permute-start.5
  130.7 4.6 collective-permute-start.4
  135.3 2.1 collective-permute-start.3
  146.5 24.0 %join_forward_3.1 = (f32[64,1536]{1,0:T(8,128)}, bf16[256,1536]{1,0:T(8,128)(2,1)}) custom-call(bf16[256,1536]{1,0:T(8,128)(2,1)} %convolution_convert_fusion.part, f32[64,1536]{1,0:T(8,128)} %get-tuple-element.78.base, f32[1,1536]{1,0:T(1,128)} %get-tuple-element.204.gain), custom_call_target="tpu_custom_call" | custom-call | tf_op jit(solution)/shard_map/join_forward_3/pallas_call | solution.py:161
  170.6 10.7 %mlp_forward_1.1 = (f32[2,256,1152]{2,1,0:T(8,128)}, bf16[256,1152]{1,0:T(8,128)(2,1)}, bf16[256,1536]{1,0:T(8,128)(2,1)}) custom-call(s32[1]{0:T(128)} %bitcast.core, bf16[256,1536]{1,0:T(8,128)(2,1)} %get-tuple-element.79.x.refs_0_, bf16[2,1536,1152]{2,1,0:T(8,128)(2,1)} %bitcast.169.own_in, bf16[2,1536,1152]{2,1,0:T(8,128)(2,1)} %collective-permute-done.1.other_in, ...), custom_call_target="tpu_custom_call" | custom-call | tf_op jit(solution)/shard_map/mlp_forward_1/pallas_call | solution.py:360
  181.2 10.4 %mlp_backward_1.1 = (bf16[2,256,1152]{2,1,0:T(8,128)(2,1)}, bf16[256,1536]{1,0:T(8,128)(2,1)}) custom-call(s32[1]{0:T(128)} %bitcast.core, bf16[256,1536]{1,0:T(8,128)(2,1)} %get-tuple-element.169.low.refs_4_, f32[2,256,1152]{2,1,0:T(8,128)} %get-tuple-element.81.gate_up, bf16[2,1536,1152]{2,1,0:T(8,128)(2,1)} %bitcast.169.own_in, ...), custom_call_target="tpu_custom_call" | custom-call | tf_op jit(solution)/shard_map/mlp_backward_1/pallas_call | solution.py:413
  191.7 2.4 dynamic-slice_bitcast_fusion.5
  194.9 2.1 constant_dynamic-slice_fusion.5
  199.4 8.6 %weight_grad_b.1 = bf16[1536,1728]{1,0:T(8,128)(2,1)} custom-call(s32[1]{0:T(128)} %bitcast.core, bf16[256,1536]{1,0:T(8,128)(2,1)} %get-tuple-element.79.x.refs_0_, bf16[256,1536]{1,0:T(8,128)(2,1)} %collective-permute-done.6.refs_1_, bf16[256,1152]{1,0:T(8,128)(2,1)} %get-tuple-element.173.refs_2_, bf16[256,1152]{1,0:T(8,128)(2,1)} %collective-permute-done.7.refs_3_, ...), custom_call_target="tpu_custom_call" | custom-call | tf_op jit(solution)/shard_map/weight_grad_b/pallas_call | solution.py:463
  211.3 26.1 %join_backward_5.1 = (f32[64,1536]{1,0:T(8,128)}, f32[1,1536]{1,0:T(1,128)}, bf16[256,1536]{1,0:T(8,128)(2,1)}) custom-call(bf16[256,1536]{1,0:T(8,128)(2,1)} %get-tuple-element.85.part, f32[64,1536]{1,0:T(8,128)} %get-tuple-element.86.base, f32[1,1536]{1,0:T(1,128)} %get-tuple-element.204.gain, f32[64,1536]{1,0:T(8,128)} %bitcast_convert_fusion.1.up), custom_call_target="tpu_custom_call" | custom-call | tf_op jit(solution)/shard_map/join_backward_5/pallas_call | solution.py:190
  237.5 2.1 convolution_convert_fusion.3
  240.4 2.6 fusion.14
  254.8 6.1 %collective-permute-done.11 = bf16[256,256]{1,0:T(8,128)(2,1)S(1)} collective-permute-done((bf16[256,256]{1,0:T(8,128)(2,1)}, bf16[256,256]{1,0:T(8,128)(2,1)S(1)}, u32[]{:S(2)}, u32[]{:S(2)}) %collective-permute-start.11) | collective-permute-done | bytes 131104 | tf_op jit(solution)/shard_map/ppermute | solution.py:740
  260.9 9.3 %collective-permute-done.10 = bf16[256,256]{1,0:T(8,128)(2,1)} collective-permute-done((bf16[256,256]{1,0:T(8,128)(2,1)}, bf16[256,256]{1,0:T(8,128)(2,1)}, u32[]{:S(2)}, u32[]{:S(2)}) %collective-permute-start.10) | collective-permute-done | bytes 131104 | tf_op jit(solution)/shard_map/ppermute | solution.py:740
  271.9 2.5 fusion.4.part
  274.4 27.2 %join_backward_6.1 = (f32[64,1536]{1,0:T(8,128)}, f32[1,1536]{1,0:T(1,128)}, bf16[256,1536]{1,0:T(8,128)(2,1)}, bf16[256,256]{1,0:T(8,128)(2,1)}) custom-call(bf16[256,1536]{1,0:T(8,128)(2,1)} %fusion.4.part, f32[64,1536]{1,0:T(8,128)} %get-tuple-element.78.base, f32[1,1536]{1,0:T(1,128)} %get-tuple-element.203.gain, f32[64,1536]{1,0:T(8,128)} %get-tuple-element.88.up, ...), custom_call_target="tpu_custom_call" | custom-call | tf_op jit(solution)/shard_map/join_backward_6/pallas_call | solution.py:190
  301.5 11.6 %mlp_backward_0.1 = (bf16[2,256,1152]{2,1,0:T(8,128)(2,1)}, bf16[256,1536]{1,0:T(8,128)(2,1)}) custom-call(s32[1]{0:T(128)} %bitcast.core, bf16[256,1536]{1,0:T(8,128)(2,1)} %get-tuple-element.89.low.refs_4_, f32[2,256,1152]{2,1,0:T(8,128)} %get-tuple-element.90.gate_up, bf16[2,1536,1152]{2,1,0:T(8,128)(2,1)} %bitcast.169.own_in, ...), custom_call_target="tpu_custom_call" | custom-call | tf_op jit(solution)/shard_map/mlp_backward_0/pallas_call | solution.py:413
  313.3 2.4 dynamic-slice_bitcast_fusion.3
  318.8 4.9 weight_grad_attention.1
  324.6 8.5 %weight_grad_a.1 = bf16[1536,1728]{1,0:T(8,128)(2,1)} custom-call(s32[1]{0:T(128)} %bitcast.core, bf16[256,1536]{1,0:T(8,128)(2,1)} %get-tuple-element.74.x.refs_0_, bf16[256,1536]{1,0:T(8,128)(2,1)} %collective-permute-done.12.refs_1_, bf16[256,1152]{1,0:T(8,128)(2,1)} %get-tuple-element.171.refs_2_, bf16[256,1152]{1,0:T(8,128)(2,1)} %copy-done.27, ...), custom_call_target="tpu_custom_call" | custom-call | tf_op jit(solution)/shard_map/weight_grad_a/pallas_call | solution.py:463
  335.3 24.8 %join_backward_7.1 = (f32[64,1536]{1,0:T(8,128)}, f32[1,1536]{1,0:T(1,128)}, bf16[256,1536]{1,0:T(8,128)(2,1)}) custom-call(bf16[256,1536]{1,0:T(8,128)(2,1)} %get-tuple-element.95.part, f32[64,1536]{1,0:T(8,128)} %get-tuple-element.76.base, f32[1,1536]{1,0:T(1,128)} %get-tuple-element.189.gain, f32[64,1536]{1,0:T(8,128)} %get-tuple-element.96.up), custom_call_target="tpu_custom_call" | custom-call | tf_op jit(solution)/shard_map/join_backward_7/pallas_call | solution.py:190
  360.2 2.5 fusion.56.gm
  362.7 4.5 rec_back_first.1
  367.2 18.6 %carry_9.1.arriving = f32[8,512]{1,0:T(8,128)} custom-call(f32[8,512]{1,0:T(8,128)} %get-tuple-element.101.edge), custom_call_target="tpu_custom_call" | custom-call | tf_op jit(solution)/shard_map/carry_9/pallas_call | solution.py:503
  385.8 5.3 rec_back_second.1
  396.1 2.7 fusion.26
  411.1 5.4 weight_grad_recurrent.1
  417.7 26.1 %join_backward_8.1 = (f32[64,1536]{1,0:T(8,128)}, f32[1,1536]{1,0:T(1,128)}, bf16[256,1536]{1,0:T(8,128)(2,1)}) custom-call(bf16[256,1536]{1,0:T(8,128)(2,1)} %fusion.5.part, f32[64,1536]{1,0:T(8,128)} %bitcast_convert_fusion.2.base, f32[1,1536]{1,0:T(1,128)} %get-tuple-element.187.gain, f32[64,1536]{1,0:T(8,128)} %get-tuple-element.108.up), custom_call_target="tpu_custom_call" | custom-call | tf_op jit(solution)/shard_map/join_backward_8/pallas_call | solution.py:190
  443.8 2.5 bitcast_convert_fusion
  450.0 13.4 %totals.1 = (f32[4,1536]{1,0:T(4,128)}, f32[8,512]{1,0:T(8,128)}) custom-call(f32[4,1536]{1,0:T(4,128)} %pad_maximum_fusion.4.gains, f32[8,512]{1,0:T(8,128)} %get-tuple-element.118.chan), custom_call_target="tpu_custom_call" | custom-call | tf_op jit(solution)/shard_map/totals/pallas_call | solution.py:287
  467.3 23.9 %join_forward_4.1 = (f32[64,1536]{1,0:T(8,128)}, bf16[256,1536]{1,0:T(8,128)(2,1)}) custom-call(bf16[256,1536]{1,0:T(8,128)(2,1)} %get-tuple-element.111.part, f32[64,1536]{1,0:T(8,128)} %get-tuple-element.86.base, f32[1,1536]{1,0:T(1,128)} %get-tuple-element.204.gain), custom_call_target="tpu_custom_call" | custom-call | tf_op jit(solution)/shard_map/join_forward_4/pallas_call | solution.py:161
  492.7 6.2 %reduce-scatter.10.cloned.1.call-done = bf16[192,1024]{1,0:T(8,128)(2,1)} async-done(((bf16[768,1024]{1,0:T(8,128)(2,1)}), bf16[192,1024]{1,0:T(8,128)(2,1)}) %reduce-scatter.10.cloned.1.call-update) | async-done | bytes 393232 | tf_op jit(solution)/shard_map/reduce_scatter | solution.py:790
  504.0 44.3 %reduce-scatter.6.cloned.1.call-done = bf16[192,1536]{1,0:T(8,128)(2,1)} async-done(((bf16[768,1536]{1,0:T(8,128)(2,1)}), bf16[192,1536]{1,0:T(8,128)(2,1)}) %reduce-scatter.6.cloned.1.call-update) | async-done | bytes 589840 | tf_op jit(solution)/shard_map/reduce_scatter | solution.py:790
  551.8 2.5 copy.104
  554.3 2.1 select_convert_fusion.1
  557.1 4.5 copy.107
  (250 shorter events, 95.3 us)
Async XLA Ops:
  7.2 60.6 %copy-start = (bf16[512,1536]{1,0:T(8,128)(2,1)S(1)}, bf16[512,1536]{1,0:T(8,128)(2,1)}, u32[]{:S(2)}) copy-start(bf16[512,1536]{1,0:T(8,128)(2,1)} %param.19) | copy-start | bytes 4718596
  7.2 439.1 %reduce-scatter.14.cloned.1.call-start = ((), (), s32[]{:S(2)}) async-start(), calls=%async_computation.9 | async-start | bytes 6881280 | tf_op jit(solution)/shard_map/reduce_scatter | solution.py:790
  14.1 77.6 %collective-permute-start.1 = (bf16[2,1536,1152]{2,1,0:T(8,128)(2,1)}, bf16[2,1536,1152]{2,1,0:T(8,128)(2,1)}, u32[]{:S(2)}, u32[]{:S(2)}) collective-permute-start(bf16[2,1536,1152]{2,1,0:T(8,128)(2,1)} %bitcast.169.own_in), channel_id=1, source_target_pairs={{0,16},{16,0},{1,17},{17,1},{2,18},{18,2},{3,19},{19,3},{4,20},{20... | collective-permute-start | bytes 21233672 | tf_op jit(solution)/shard_map/ppermute | solution.py:744
  14.6 31.4 %collective-permute-start = (f32[2,1536]{1,0:T(2,128)S(1)}, f32[2,1536]{1,0:T(2,128)S(1)}, u32[]{:S(2)}, u32[]{:S(2)}) collective-permute-start(f32[2,1536]{1,0:T(2,128)S(1)} %bitcast.189), channel_id=1, source_target_pairs={{0,16},{16,0},{1,17},{17,1},{2,18},{18,2},{3,19},{19,3},{4,20},{20... | collective-permute-start | bytes 36872 | tf_op jit(solution)/shard_map/ppermute | solution.py:744
  14.6 77.0 %collective-permute-start.2 = (bf16[1152,1536]{1,0:T(8,128)(2,1)}, bf16[1152,1536]{1,0:T(8,128)(2,1)}, u32[]{:S(2)}, u32[]{:S(2)}) collective-permute-start(bf16[1152,1536]{1,0:T(8,128)(2,1)} %bitcast.17.own_out), channel_id=1, source_target_pairs={{0,16},{16,0},{1,17},{17,1},{2,18},{18,2},{3,19},{19,3},{4,20},{20... | collective-permute-start | bytes 10616840 | tf_op jit(solution)/shard_map/ppermute | solution.py:744
  25.9 9.7 %copy-start.33 = (bf16[16,1536]{1,0:T(8,128)(2,1)S(1)}, bf16[16,1536]{1,0:T(8,128)(2,1)}, u32[]{:S(2)}) copy-start(bf16[16,1536]{1,0:T(8,128)(2,1)} %get-tuple-element.69) | copy-start | bytes 147460
  27.4 8.5 %copy-start.18 = (bf16[2,256,1536]{2,1,0:T(8,128)(2,1)S(1)}, bf16[2,256,1536]{2,1,0:T(8,128)(2,1)}, u32[]{:S(2)}) copy-start(bf16[2,256,1536]{2,1,0:T(8,128)(2,1)} %param.25) | copy-start | bytes 4718596
  46.8 17.1 %copy-start.10 = (bf16[272,1536]{1,0:T(8,128)(2,1)}, bf16[272,1536]{1,0:T(8,128)(2,1)S(1)}, u32[]{:S(2)}) copy-start(bf16[272,1536]{1,0:T(8,128)(2,1)S(1)} %fusion.9) | copy-start | bytes 2506756
  91.7 34.3 %copy-start.13 = (bf16[1536,256]{1,0:T(8,128)(2,1)S(1)}, bf16[1536,256]{1,0:T(8,128)(2,1)}, u32[]{:S(2)}) copy-start(bf16[1536,256]{1,0:T(8,128)(2,1)} %param.21) | copy-start | bytes 2359300
  125.9 11.5 %copy-start.6 = (bf16[256,1536]{1,0:T(8,128)(2,1)S(1)}, bf16[256,1536]{1,0:T(8,128)(2,1)}, u32[]{:S(2)}) copy-start(bf16[256,1536]{1,0:T(8,128)(2,1)} %get-tuple-element.77.refs_0_.refs_4_) | copy-start | bytes 2359300
  127.5 14.4 %copy-start.31 = (pred[256,1024]{0,1:T(8,128)(4,1)S(1)}, pred[256,1024]{0,1:T(8,128)(4,1)}, u32[]{:S(2)}) copy-start(pred[256,1024]{0,1:T(8,128)(4,1)} %fusion.25) | copy-start | bytes 786436
  127.5 11.9 %collective-permute-start.5 = (bf16[256,256]{1,0:T(8,128)(2,1)S(1)}, bf16[256,256]{1,0:T(8,128)(2,1)S(1)}, u32[]{:S(2)}, u32[]{:S(2)}) collective-permute-start(bf16[256,256]{1,0:T(8,128)(2,1)S(1)} %convolution_convert_fusion.5), channel_id=1, source_target_pairs={{0,4},{4,8},{8,12},{1,5},{5,9},{9,13},{2,6},{6,10},{10,14},{3,7},{... | collective-permute-start | bytes 393224 | tf_op jit(solution)/shard_map/ppermute | solution.py:740
  130.7 8.8 %collective-permute-start.4 = (bf16[256,256]{1,0:T(8,128)(2,1)S(1)}, bf16[256,256]{1,0:T(8,128)(2,1)S(1)}, u32[]{:S(2)}, u32[]{:S(2)}) collective-permute-start(bf16[256,256]{1,0:T(8,128)(2,1)S(1)} %convolution_convert_fusion.5), channel_id=1, source_target_pairs={{0,8},{4,12},{1,9},{5,13},{2,10},{6,14},{3,11},{7,15},{16,24},{20,... | collective-permute-start | bytes 393224 | tf_op jit(solution)/shard_map/ppermute | solution.py:740
  135.3 5.5 collective-permute-start.3
  141.9 101.1 %copy-start.16 = (bf16[1024,256]{1,0:T(8,128)(2,1)}, bf16[1024,256]{1,0:T(8,128)(2,1)S(1)}, u32[]{:S(2)}) copy-start(bf16[1024,256]{1,0:T(8,128)(2,1)S(1)} %pad_maximum_fusion.2) | copy-start | bytes 1572868
  170.4 28.9 %collective-permute-start.6 = (bf16[256,1536]{1,0:T(8,128)(2,1)}, bf16[256,1536]{1,0:T(8,128)(2,1)}, u32[]{:S(2)}, u32[]{:S(2)}) collective-permute-start(bf16[256,1536]{1,0:T(8,128)(2,1)} %get-tuple-element.79.x.refs_0_), channel_id=1, source_target_pairs={{0,16},{16,0},{1,17},{17,1},{2,18},{18,2},{3,19},{19,3},{4,20},{20... | collective-permute-start | bytes 2359304 | tf_op jit(solution)/shard_map/ppermute | solution.py:744
  194.1 5.3 collective-permute-start.7
  197.0 1.6 collective-permute-start.8
  208.0 238.3 %reduce-scatter.12.cloned.1.call-start = ((), (), s32[]{:S(2)}) async-start(), calls=%async_computation.8 | async-start | bytes 6881280 | tf_op jit(solution)/shard_map/reduce_scatter | solution.py:790
  210.0 113.8 %collective-permute-start.12 = (bf16[256,1536]{1,0:T(8,128)(2,1)}, bf16[256,1536]{1,0:T(8,128)(2,1)}, u32[]{:S(2)}, u32[]{:S(2)}) collective-permute-start(bf16[256,1536]{1,0:T(8,128)(2,1)} %get-tuple-element.74.x.refs_0_), channel_id=1, source_target_pairs={{0,16},{16,0},{1,17},{17,1},{2,18},{18,2},{3,19},{19,3},{4,20},{20... | collective-permute-start | bytes 2359304 | tf_op jit(solution)/shard_map/ppermute | solution.py:744
  210.1 105.6 %collective-permute-start.16 = (bf16[256,1536]{1,0:T(8,128)(2,1)S(1)}, bf16[256,1536]{1,0:T(8,128)(2,1)}, u32[]{:S(2)}, u32[]{:S(2)}) collective-permute-start(bf16[256,1536]{1,0:T(8,128)(2,1)S(1)} %copy-done.6), channel_id=1, source_target_pairs={{0,16},{16,0},{1,17},{17,1},{2,18},{18,2},{3,19},{19,3},{4,20},{20... | collective-permute-start | bytes 2359304 | tf_op jit(solution)/shard_map/ppermute | solution.py:744
  246.3 14.7 %collective-permute-start.11 = (bf16[256,256]{1,0:T(8,128)(2,1)}, bf16[256,256]{1,0:T(8,128)(2,1)S(1)}, u32[]{:S(2)}, u32[]{:S(2)}) collective-permute-start(bf16[256,256]{1,0:T(8,128)(2,1)} %get-tuple-element.181), channel_id=1, source_target_pairs={{12,0},{13,1},{14,2},{15,3},{28,16},{29,17},{30,18},{31,19}} | collective-permute-start | bytes 393224 | tf_op jit(solution)/shard_map/ppermute | solution.py:740
  247.6 22.7 %collective-permute-start.10 = (bf16[256,256]{1,0:T(8,128)(2,1)}, bf16[256,256]{1,0:T(8,128)(2,1)}, u32[]{:S(2)}, u32[]{:S(2)}) collective-permute-start(bf16[256,256]{1,0:T(8,128)(2,1)} %get-tuple-element.182), channel_id=1, source_target_pairs={{8,0},{12,4},{9,1},{13,5},{10,2},{14,6},{11,3},{15,7},{24,16},{28,... | collective-permute-start | bytes 393224 | tf_op jit(solution)/shard_map/ppermute | solution.py:740
  248.9 21.5 %collective-permute-start.9 = (bf16[256,256]{1,0:T(8,128)(2,1)}, bf16[256,256]{1,0:T(8,128)(2,1)}, u32[]{:S(2)}, u32[]{:S(2)}) collective-permute-start(bf16[256,256]{1,0:T(8,128)(2,1)} %get-tuple-element.180), channel_id=1, source_target_pairs={{4,0},{8,4},{12,8},{5,1},{9,5},{13,9},{6,2},{10,6},{14,10},{7,3},{... | collective-permute-start | bytes 393224 | tf_op jit(solution)/shard_map/ppermute | solution.py:740
  254.8 17.1 %copy-start.7 = (f32[256,1536]{1,0:T(8,128)S(1)}, f32[256,1536]{1,0:T(8,128)}, u32[]{:S(2)}) copy-start(f32[256,1536]{1,0:T(8,128)} %fusion.55) | copy-start | bytes 4718596
  260.9 9.4 %copy-start.35 = (bf16[256,256]{1,0:T(8,128)(2,1)}, bf16[256,256]{1,0:T(8,128)(2,1)S(1)}, u32[]{:S(2)}) copy-start(bf16[256,256]{1,0:T(8,128)(2,1)S(1)} %collective-permute-done.11) | copy-start | bytes 393220
  260.9 52.3 %collective-permute-start.20 = (bf16[256,384]{1,0:T(8,128)(2,1)}, bf16[256,384]{1,0:T(8,128)(2,1)}, u32[]{:S(2)}, u32[]{:S(2)}) collective-permute-start(bf16[256,384]{1,0:T(8,128)(2,1)} %copy.94.refs_10_), channel_id=1, source_target_pairs={{0,16},{16,0},{1,17},{17,1},{2,18},{18,2},{3,19},{19,3},{4,20},{20... | collective-permute-start | bytes 589832 | tf_op jit(solution)/shard_map/ppermute | solution.py:744
  270.2 48.3 %collective-permute-start.19 = (bf16[256,1536]{1,0:T(8,128)(2,1)}, bf16[256,1536]{1,0:T(8,128)(2,1)}, u32[]{:S(2)}, u32[]{:S(2)}) collective-permute-start(bf16[256,1536]{1,0:T(8,128)(2,1)} %get-tuple-element.87.refs_8_), channel_id=1, source_target_pairs={{0,16},{16,0},{1,17},{17,1},{2,18},{18,2},{3,19},{19,3},{4,20},{20... | collective-permute-start | bytes 2359304 | tf_op jit(solution)/shard_map/ppermute | solution.py:744
  270.4 45.7 %collective-permute-start.17 = (bf16[256,384]{1,0:T(8,128)(2,1)}, bf16[256,384]{1,0:T(8,128)(2,1)}, u32[]{:S(2)}, u32[]{:S(2)}) collective-permute-start(bf16[256,384]{1,0:T(8,128)(2,1)} %copy.93.refs_2_), channel_id=1, source_target_pairs={{0,16},{16,0},{1,17},{17,1},{2,18},{18,2},{3,19},{19,3},{4,20},{20... | collective-permute-start | bytes 589832 | tf_op jit(solution)/shard_map/ppermute | solution.py:744
  301.5 11.7 %copy-start.14 = (bf16[256,1536]{1,0:T(8,128)(2,1)S(1)}, bf16[256,1536]{1,0:T(8,128)(2,1)}, u32[]{:S(2)}) copy-start(bf16[256,1536]{1,0:T(8,128)(2,1)} %get-tuple-element.89.low.refs_4_) | copy-start | bytes 2359300
  313.2 10.6 %collective-permute-start.14 = (bf16[256,1536]{1,0:T(8,128)(2,1)S(1)}, bf16[256,1536]{1,0:T(8,128)(2,1)}, u32[]{:S(2)}, u32[]{:S(2)}) collective-permute-start(bf16[256,1536]{1,0:T(8,128)(2,1)S(1)} %copy-done.14), channel_id=1, source_target_pairs={{0,16},{16,0},{1,17},{17,1},{2,18},{18,2},{3,19},{19,3},{4,20},{20... | collective-permute-start | bytes 2359304 | tf_op jit(solution)/shard_map/ppermute | solution.py:744
  315.7 8.0 %collective-permute-start.13 = (bf16[256,1152]{1,0:T(8,128)(2,1)}, bf16[256,1152]{1,0:T(8,128)(2,1)S(1)}, u32[]{:S(2)}, u32[]{:S(2)}) collective-permute-start(bf16[256,1152]{1,0:T(8,128)(2,1)} %get-tuple-element.170), channel_id=1, source_target_pairs={{0,16},{16,0},{1,17},{17,1},{2,18},{18,2},{3,19},{19,3},{4,20},{20... | collective-permute-start | bytes 1769480 | tf_op jit(solution)/shard_map/ppermute | solution.py:744
  316.1 2.0 collective-permute-start.18
  318.1 5.6 collective-permute-start.15
  333.1 132.5 %reduce-scatter.8.cloned.1.call-start = ((), (), s32[]{:S(2)}) async-start(), calls=%async_computation.6 | async-start | bytes 163840 | tf_op jit(solution)/shard_map/reduce_scatter | solution.py:790
  334.3 28.4 %copy-start.4 = (bf16[256,1536]{1,0:T(8,128)(2,1)}, bf16[256,1536]{1,0:T(8,128)(2,1)S(1)}, u32[]{:S(2)}) copy-start(bf16[256,1536]{1,0:T(8,128)(2,1)S(1)} %slice.151.refs_0_.refs_4_) | copy-start | bytes 2359300
  334.3 75.9 %collective-permute-start.26 = (bf16[256,512]{1,0:T(8,128)(2,1)}, bf16[256,512]{1,0:T(8,128)(2,1)}, u32[]{:S(2)}, u32[]{:S(2)}) collective-permute-start(bf16[256,512]{1,0:T(8,128)(2,1)} %get-tuple-element.162.refs_10_), channel_id=1, source_target_pairs={{0,16},{16,0},{1,17},{17,1},{2,18},{18,2},{3,19},{19,3},{4,20},{20... | collective-permute-start | bytes 786440 | tf_op jit(solution)/shard_map/ppermute | solution.py:744
  334.8 75.5 %collective-permute-start.22 = (bf16[256,1536]{1,0:T(8,128)(2,1)S(1)}, bf16[256,1536]{1,0:T(8,128)(2,1)S(1)}, u32[]{:S(2)}, u32[]{:S(2)}) collective-permute-start(bf16[256,1536]{1,0:T(8,128)(2,1)S(1)} %slice.151.refs_0_.refs_4_), channel_id=1, source_target_pairs={{0,16},{16,0},{1,17},{17,1},{2,18},{18,2},{3,19},{19,3},{4,20},{20... | collective-permute-start | bytes 2359304 | tf_op jit(solution)/shard_map/ppermute | solution.py:744
  334.9 66.1 %collective-permute-start.28 = (bf16[256,512]{1,0:T(8,128)(2,1)}, bf16[256,512]{1,0:T(8,128)(2,1)}, u32[]{:S(2)}, u32[]{:S(2)}) collective-permute-start(bf16[256,512]{1,0:T(8,128)(2,1)} %get-tuple-element.102.conv), channel_id=1, source_target_pairs={{0,16},{16,0},{1,17},{17,1},{2,18},{18,2},{3,19},{19,3},{4,20},{20... | collective-permute-start | bytes 786440 | tf_op jit(solution)/shard_map/ppermute | solution.py:744
  360.1 50.2 %collective-permute-start.25 = (bf16[256,1536]{1,0:T(8,128)(2,1)}, bf16[256,1536]{1,0:T(8,128)(2,1)}, u32[]{:S(2)}, u32[]{:S(2)}) collective-permute-start(bf16[256,1536]{1,0:T(8,128)(2,1)} %get-tuple-element.97.refs_8_), channel_id=1, source_target_pairs={{0,16},{16,0},{1,17},{17,1},{2,18},{18,2},{3,19},{19,3},{4,20},{20... | collective-permute-start | bytes 2359304 | tf_op jit(solution)/shard_map/ppermute | solution.py:744
  391.8 8.9 %collective-permute-start.21 = (f32[3,512]{1,0:T(4,128)S(1)}, f32[3,512]{1,0:T(4,128)S(1)}, u32[]{:S(2)}, u32[]{:S(2)}) collective-permute-start(f32[3,512]{1,0:T(4,128)S(1)} %slice.138), channel_id=1, source_target_pairs={{4,0},{8,4},{12,8},{5,1},{9,5},{13,9},{6,2},{10,6},{14,10},{7,3},{... | collective-permute-start | bytes 18440 | tf_op jit(solution)/shard_map/ppermute | solution.py:740
  400.8 1.6 collective-permute-start.27
  401.0 9.3 %collective-permute-start.24 = (bf16[256,512]{1,0:T(8,128)(2,1)}, bf16[256,512]{1,0:T(8,128)(2,1)}, u32[]{:S(2)}, u32[]{:S(2)}) collective-permute-start(bf16[256,512]{1,0:T(8,128)(2,1)} %get-tuple-element.105.refs_6_), channel_id=1, source_target_pairs={{0,16},{16,0},{1,17},{17,1},{2,18},{18,2},{3,19},{19,3},{4,20},{20... | collective-permute-start | bytes 786440 | tf_op jit(solution)/shard_map/ppermute | solution.py:744
  403.1 7.2 %collective-permute-start.23 = (bf16[256,512]{1,0:T(8,128)(2,1)S(1)}, bf16[256,512]{1,0:T(8,128)(2,1)}, u32[]{:S(2)}, u32[]{:S(2)}) collective-permute-start(bf16[256,512]{1,0:T(8,128)(2,1)S(1)} %pad_maximum_fusion.3.refs_2_), channel_id=1, source_target_pairs={{0,16},{16,0},{1,17},{17,1},{2,18},{18,2},{3,19},{19,3},{4,20},{20... | collective-permute-start | bytes 786440 | tf_op jit(solution)/shard_map/ppermute | solution.py:744
  416.6 82.4 %reduce-scatter.10.cloned.1.call-start = ((), (), s32[]{:S(2)}) async-start(), calls=%async_computation.7 | async-start | bytes 1966080 | tf_op jit(solution)/shard_map/reduce_scatter | solution.py:790
  417.1 131.1 %reduce-scatter.6.cloned.1.call-start = ((), (), s32[]{:S(2)}) async-start(), calls=%async_computation.5 | async-start | bytes 2949120 | tf_op jit(solution)/shard_map/reduce_scatter | solution.py:790
  449.3 102.5 %collective-permute-start.30 = (bf16[384,1728]{0,1:T(8,128)(2,1)}, bf16[384,1728]{0,1:T(8,128)(2,1)}, u32[]{:S(2)}, u32[]{:S(2)}) collective-permute-start(bf16[384,1728]{0,1:T(8,128)(2,1)} %copy.103), channel_id=1, source_target_pairs={{0,16},{16,0},{1,17},{17,1},{2,18},{18,2},{3,19},{19,3},{4,20},{20... | collective-permute-start | bytes 3981320 | tf_op jit(solution)/shard_map/ppermute | solution.py:744
  466.3 24.9 %collective-permute-start.29 = (bf16[16,512]{1,0:T(8,128)(2,1)S(1)}, bf16[16,512]{1,0:T(8,128)(2,1)S(1)}, u32[]{:S(2)}, u32[]{:S(2)}) collective-permute-start(bf16[16,512]{1,0:T(8,128)(2,1)S(1)} %dynamic-slice_bitcast_fusion.9), channel_id=1, source_target_pairs={{0,16},{16,0},{1,17},{17,1},{2,18},{18,2},{3,19},{19,3},{4,20},{20... | collective-permute-start | bytes 49160 | tf_op jit(solution)/shard_map/ppermute | solution.py:744
  (34 other events, 96.5 us)
Sparse Core Ops, SparseCore 0:
  208.1 110.3 reduce-scatter.13
  333.3 106.3 reduce-scatter.11
  442.5 20.3 reduce-scatter.7
  465.6 33.2 reduce-scatter.9
  501.6 46.5 reduce-scatter.5
